TPU v7x, 128 devices: a whole 4x4x4 slice. The times are simulated.
128 devices in a mesh: dp: 8 (over y_lo, x), tensor: 16 (over y_hi, z, core).
Axes of the slice: x: 4, y: 4 (y_hi: 2, y_lo: 2; y = y_hi * 2 + y_lo), z: 4, core: 2. Of those that a mesh axis runs over, the one named last changes fastest.
Arguments:
- tokens: bfloat16 [8192, 4096], P(('dp', 'tensor')), parts along dimension 0, may hold values from -6 to 6
- norm_gain: float32 [4096], replicated, may hold values from 0.5 to 1.5
- gate_weight: bfloat16 [4096, 14336], P(None, 'tensor'), may hold values from -0.09375 to 0.09375
- up_weight: bfloat16 [4096, 14336], P(None, 'tensor'), may hold values from -0.09375 to 0.09375
- down_weight: bfloat16 [14336, 4096], P('tensor'), may hold values from -0.0625 to 0.0625
Outputs:
- mixed: bfloat16 [8192, 4096], P('dp', 'tensor'), parts along dimension 0
There are 8 independent parts, one for each index of `dp`. A program takes and returns all parts, laid end to end along the dimension named above; an argument that names none is the same for every part. Nothing has to cross between parts.
All inputs are finite; a program needn't handle non-finite values.
Results may differ from a plain program's by a relative error of at most 0.0053.
Values may be sent and summed in bfloat16 or wider, within the bound.
A program may use at most 128 MiB of HBM per device.

v0:
```python
import jax
import jax.numpy as jnp
from jax import lax
from jax.sharding import PartitionSpec as P


def on_device(tokens, norm_gain, gate_weight, up_weight, down_weight):
    wide = tokens.astype(jnp.float32)
    square_mean = jnp.mean(wide * wide, axis=1, keepdims=True)
    normed = (wide * norm_gain[None, :] / jnp.sqrt(square_mean + 1e-05)).astype(jnp.bfloat16)
    piece = lax.all_gather(normed, "tensor", axis=0, tiled=True)
    gate = jnp.dot(piece, gate_weight, preferred_element_type=jnp.float32)
    up = jnp.dot(piece, up_weight, preferred_element_type=jnp.float32)
    hidden = (jax.nn.silu(gate) * up).astype(jnp.bfloat16)
    residual = lax.all_to_all(tokens, "tensor", split_axis=1, concat_axis=0, tiled=True)
    summed = lax.psum_scatter(
        jnp.einsum("fc,tf->ct", down_weight, hidden, preferred_element_type=jnp.float32),
        "tensor",
        scatter_dimension=0,
        tiled=True,
    )
    return (residual.astype(jnp.float32) + summed.T).astype(jnp.bfloat16)


def solution(mesh):
    return jax.shard_map(
        on_device,
        mesh=mesh,
        in_specs=(
            P(("dp", "tensor"), None),
            P(),
            P(None, "tensor"),
            P(None, "tensor"),
            P("tensor", None),
        ),
        out_specs=P("dp", "tensor"),
        check_vma=False,
    )
```

profile of v0, /device:TPU:0, one launch (start us, length us, event | category | flops | bytes accessed | tf_op | source)
XLA Modules:
  0.0 281.8 jit_solution(14501327562097378048)
XLA Ops:
  6.5 0.0 all-gather.2.cloned.1.call-start
  6.5 1.2 fusion.3
  7.8 2.0 fusion.2
  9.8 0.0 all-gather.2.cloned.1.call-update
  9.8 0.0 reduce-scatter.2.cloned.1.call-start
  9.9 75.4 %all-gather.2.cloned.1.call-done = bf16[1024,4096]{1,0:T(8,128)(2,1)} async-done(((bf16[64,4096]{1,0:T(8,128)(2,1)}), bf16[1024,4096]{1,0:T(8,128)(2,1)}) %all-gather.2.cloned.1.call-update) | async-done | bytes 8388624 | tf_op jit(solution)/shard_map/all_gather | solution.py:11
  85.3 14.6 %fusion.6 = f32[1024,896]{1,0:T(8,128)} fusion(bf16[1024,4096]{1,0:T(8,128)(2,1)} %all-gather.2.cloned.1.call-done, bf16[4096,896]{1,0:T(8,128)(2,1)} %param.7), kind=kOutput, calls=%fused_computation.13 | convolution fusion | flops 7516192768 | bytes 19398656 | tf_op jit(solution)/shard_map/dot_general | solution.py:12
  99.9 27.9 %convolution_bitcast_fusion = f32[4096,1024]{0,1:T(8,128)} fusion(bf16[896,4096]{1,0:T(8,128)(2,1)} %param.9, f32[1024,896]{1,0:T(8,128)} %fusion.6, bf16[1024,4096]{1,0:T(8,128)(2,1)} %all-gather.2.cloned.1.call-done, bf16[4096,896]{1,0:T(8,128)(2,1)} %param.8), kind=kOutput, calls=%fused_computation | convolution fusion | flops 15037890560 | bytes 43515904 | tf_op jit(solution)/shard_map/fc,tf->ct/dot_general | solution.py:17
  127.8 0.0 copy-start
  127.8 0.0 reduce-scatter.2.cloned.1.call-update
  127.8 1.0 copy-done
  128.9 15.0 %all_to_all.13 = bf16[64,16,256]{2,0,1:T(8,128)(2,1)S(1)} all-to-all(bf16[64,16,256]{2,0,1:T(8,128)(2,1)S(1)} %bitcast.20), channel_id=1, replica_groups=mesh['dp'=8,'tensor'=16] {'tensor'}, dimensions={1} | all-to-all | bytes 1048576 | tf_op jit(solution)/shard_map/all_to_all | solution.py:15
  143.8 129.0 %reduce-scatter.2.cloned.1.call-done = f32[256,1024]{0,1:T(8,128)} async-done(((f32[4096,1024]{0,1:T(8,128)}), f32[256,1024]{0,1:T(8,128)}) %reduce-scatter.2.cloned.1.call-update) | async-done | bytes 1048592 | tf_op jit(solution)/shard_map/reduce_scatter | solution.py:16
  272.8 2.1 fusion.4
  (2 shorter events, 0.1 us)
Async XLA Ops:
  6.5 78.7 %all-gather.2.cloned.1.call-start = ((), (), s32[]{:S(2)}) async-start(), calls=%async_computation.2 | async-start | bytes 8912896 | tf_op jit(solution)/shard_map/all_gather | solution.py:11
  9.8 263.0 %reduce-scatter.2.cloned.1.call-start = ((), (), s32[]{:S(2)}) async-start(), calls=%async_computation.3 | async-start | bytes 17825792 | tf_op jit(solution)/shard_map/reduce_scatter | solution.py:16
  127.8 1.0 copy-start
Sparse Core Ops, SparseCore 0:
  9.9 75.3 all-gather.1
  127.9 144.8 reduce-scatter.1
where the time goes:
time: 282 us
  waiting for transfers between devices  204 us (72%)
  matrix products  42.5 us (15%)
  blocking collectives  15 us (5%)
  between operations  13.4 us (5%)
  other arithmetic  5.37 us (2%)
    reduce_scatter x1, waiting for transfers between devices, on_device(): lax.psum_scatter(jnp.einsum('fc,tf->ct', down_weight, hidden, preferred_e...  129 us
    all_gather x1, waiting for transfers between devices, on_device(): piece = lax.all_gather(normed, 'tensor', axis=0, tiled=True)  75.4 us
    dot_general x1, matrix products, on_device(): jnp.einsum('fc,tf->ct', down_weight, hidden, preferred_element_type=jnp.f...  27.9 us
    all_to_all x1, blocking collectives, on_device(): lax.all_to_all(tokens, 'tensor', split_axis=1, concat_axis=0, tiled=True)  15 us
    dot_general x1, matrix products, on_device(): gate = jnp.dot(piece, gate_weight, preferred_element_type=jnp.float32)  14.6 us
  transfers between devices with their start and end apart: 2, of which 2 were waited for; matrix products, arithmetic and copies ran while one was open for 0% of the time, Pallas kernels for 0%

commit v1 on v0

v1 whole, which is shorter than its diff:
```python
import jax
import jax.numpy as jnp
from jax import lax
from jax.experimental import pallas as pl
from jax.experimental.pallas import tpu as pltpu
from jax.sharding import PartitionSpec as P

MESH = pl.DeviceIdType.MESH
F32, BF16 = jnp.float32, jnp.bfloat16
D, F, ROWS, COLS = 4096, 896, 1024, 256

SLOTS = [(0, 0), (0, 1), (0, 3), (1, 0), (0, 2), (1, 1), (1, 3), (1, 2)]
DESTS = [(1, 2), (1, 1), (1, 3), (0, 2), (1, 0), (0, 1), (0, 3), (0, 0)]
SLOT = {b: i for i, b in enumerate(SLOTS)}
DEST = {b: i for i, b in enumerate(DESTS)}
CHUNKS = {"A": (0, 1), "B": (1, 2), "C": (3, 2), "D": (5, 2), "E": (7, 1)}
PIECES = [(0, 3), (3, 2), (5, 3)]
SEEN = {
    "zp": lambda q, k: (q, (k + 1) % 4),
    "zm": lambda q, k: (q, (k + 3) % 4),
    "y": lambda q, k: (1 - q, k),
}


def kernel(tok_hbm, gain_ref, gate_hbm, up_hbm, down_hbm, out_hbm,
           x, w, dn, res, hid, own, sb, rb, sd, yl, zl, zh, yf, zf, out,
           local_sem, out_sem, bar_unused, ss, rs):
    dp, t = lax.axis_index("dp"), lax.axis_index("tensor")
    hi, z, c = t // 8, lax.rem(t // 2, 4), lax.rem(t, 2)

    def member(q, k, core):
        return (hi if q == 0 else 1 - hi) * 8 + lax.rem(z + k, 4) * 2 + core

    peer = {
        "zp": (dp, member(0, 1, c)),
        "zm": (dp, member(0, 3, c)),
        "y": (dp, member(1, 0, c)),
        "s": (dp, member(0, 0, 1 - c)),
    }

    mine = pl.ds(pl.multiple_of(c * 64, 64), 64)
    other = pl.ds(pl.multiple_of((1 - c) * 64, 64), 64)
    tok_copy = pltpu.make_async_copy(tok_hbm, res.at[mine], local_sem.at[0])
    tok_copy.start()
    w_copies, d_copies = [], []
    for j in range(7):
        for part, src in enumerate((gate_hbm, up_hbm)):
            w_copies.append(pltpu.make_async_copy(
                src.at[:, pl.ds(j * 128, 128)], w.at[:, pl.ds(j * 256 + part * 128, 128)],
                local_sem.at[1 + 2 * j + part]))
    for r, (q, k) in enumerate(DESTS):
        for part, core in enumerate((1 - c, c)):
            col = pl.multiple_of(member(q, k, core) * COLS, COLS)
            d_copies.append(pltpu.make_async_copy(
                down_hbm.at[:, pl.ds(col, COLS)], dn.at[:, pl.ds((2 * r + part) * COLS, COLS)],
                local_sem.at[15 + 2 * r + part]))
    for copy in w_copies + d_copies:
        copy.start()

    barrier = pltpu.get_barrier_semaphore()
    for link in ("zp", "zm", "y", "s"):
        pl.semaphore_signal(barrier, inc=1, device_id=peer[link], device_id_type=MESH)

    count = [0]

    def remote(link, src, dst):
        i = count[0]
        count[0] += 1
        return pltpu.make_async_remote_copy(
            src_ref=src, dst_ref=dst, send_sem=ss.at[i], recv_sem=rs.at[i],
            device_id=peer[link], device_id_type=MESH)

    started = []

    def start(copy):
        copy.start()
        started.append(copy)

    def rows_of(block, h):
        return pl.ds(pl.multiple_of(SLOT[block] * 128 + c * 64 + h * 32, 32), 32)

    def gather(link, src, dst, h):
        return remote(link, x.at[rows_of(src, h)], x.at[rows_of(dst, h)])

    zp0 = [gather("zp", (0, 0), (0, 3), h) for h in range(2)]
    zm0 = [gather("zm", (0, 0), (0, 1), h) for h in range(2)]
    y0 = [gather("y", (0, 0), (1, 0), h) for h in range(2)]
    zp2 = gather("zp", (0, 3), (0, 2), 0)
    zm2 = gather("zm", (0, 1), (0, 2), 1)
    zpp = [gather("zp", (1, 0), (1, 3), h) for h in range(2)]
    zmp = [gather("zm", (1, 0), (1, 1), h) for h in range(2)]
    y2 = [gather("y", (0, 2), (1, 2), h) for h in range(2)]
    sib = {b: [gather("s", b, b, h) for h in range(2)] for b in SLOTS}

    def pair(chunk, first, last):
        lo, n = CHUNKS[chunk]
        part = (pl.ds(first, last - first), pl.ds(lo * 128, n * 128))
        return remote("s", sb.at[part], rb.at[part])

    pairs = {}
    for name in CHUNKS:
        pairs[name] = [pair(name, 0, 3), pair(name, 3, 8)]
    leaf = {}
    for name, (lo, n) in CHUNKS.items():
        part = pl.ds(lo * 128, n * 128)
        leaf[name] = {
            "y": remote("y", sd.at[DEST[1, 2], part], yl.at[part]),
            "zp": remote("zp", sd.at[DEST[1, 1], part], zl.at[0, part]),
            "zm": remote("zm", sd.at[DEST[1, 3], part], zl.at[1, part]),
        }
    half, across, last = [], [], []
    for lo, n in PIECES:
        part = pl.ds(lo * 128, n * 128)
        half.append({
            "zp": remote("zp", sd.at[DEST[0, 2], part, pl.ds(0, 128)], zh.at[0, part]),
            "zm": remote("zm", sd.at[DEST[0, 2], part, pl.ds(128, 128)], zh.at[1, part]),
        })
        across.append(remote("y", sd.at[DEST[1, 0], part], yf.at[part]))
        last.append({
            "zp": remote("zp", sd.at[DEST[0, 1], part], zf.at[0, part]),
            "zm": remote("zm", sd.at[DEST[0, 3], part], zf.at[1, part]),
        })

    waited = set()

    def arrived(copy):
        if id(copy) not in waited:
            waited.add(id(copy))
            copy.wait_recv()

    def leaf_with(link, slot):
        s = SLOT[SEEN[link](*SLOTS[slot])]
        for name, (lo, n) in CHUNKS.items():
            if lo <= s < lo + n:
                arrived(leaf[name][link])
        return pl.ds(s * 128, 128)

    def piece_with(link, messages, slot):
        s = SLOT[SEEN[link](*SLOTS[slot])]
        for i, (lo, n) in enumerate(PIECES):
            if lo <= s < lo + n:
                arrived(messages[i] if link == "y" else messages[i][link])
        return pl.ds(s * 128, 128)

    res[other] = jnp.zeros((64, D), BF16)
    tok_copy.wait()
    gain = gain_ref[...]
    for i in range(4):
        wide = res[pl.ds(pl.multiple_of(c * 64 + i * 16, 16), 16)].astype(F32)
        square_mean = jnp.mean(wide * wide, axis=1, keepdims=True)
        normed = wide * gain / jnp.sqrt(square_mean + 1e-05)
        x[pl.ds(pl.multiple_of(c * 64 + i * 16, 16), 16)] = normed.astype(BF16)
    pl.semaphore_wait(barrier, 4)

    for copy in (zp0[0], zm0[1], y0[0], sib[0, 0][0], sib[0, 0][1], zp0[1], zm0[0], y0[1]):
        start(copy)

    def dot_in(name):
        lo, n = CHUNKS[name]
        rows = pl.ds(lo * 128, n * 128)
        both = jnp.dot(x[rows], w[...], preferred_element_type=F32)
        for j in range(7):
            gate, up = both[:, j * 256:j * 256 + 128], both[:, j * 256 + 128:j * 256 + 256]
            hid[rows, pl.ds(j * 128, 128)] = (gate / (1.0 + jnp.exp(-gate)) * up).astype(BF16)

    def dot_out(name, first, last):
        lo, n = CHUNKS[name]
        rows = pl.ds(lo * 128, n * 128)
        part = jnp.dot(hid[rows], dn[:, pl.ds(first * 512, (last - first) * 512)], preferred_element_type=F32)
        for r in range(first, last):
            for side in range(2):
                at = (r - first) * 512 + side * 256
                value = part[:, at:at + 256]
                if name == "A":
                    core = (1 - c, c)[side]
                    col = pl.multiple_of(member(*DESTS[r], core) * COLS, COLS)
                    value = value + res[:, pl.ds(col, COLS)].astype(F32)
                if side == 0:
                    sb[r, rows] = value.astype(BF16)
                else:
                    own[r, rows] = value

    def chip_sum(r, slot):
        rows = pl.ds(slot * 128, 128)
        return own[r, rows] + rb[r, rows].astype(F32)

    def send_leaf(name):
        lo, n = CHUNKS[name]
        arrived(pairs[name][0])
        for link, dest in (("y", (1, 2)), ("zp", (1, 1)), ("zm", (1, 3))):
            r = DEST[dest]
            for slot in range(lo, lo + n):
                sd[r, pl.ds(slot * 128, 128)] = chip_sum(r, slot).astype(BF16)
            start(leaf[name][link])

    def pair_rest(lo, n):
        for name, (a, m) in CHUNKS.items():
            if a < lo + n and lo < a + m:
                arrived(pairs[name][1])

    def send_half(i):
        lo, n = PIECES[i]
        pair_rest(lo, n)
        r = DEST[0, 2]
        for slot in range(lo, lo + n):
            got = leaf_with("y", slot)
            sd[r, pl.ds(slot * 128, 128)] = (chip_sum(r, slot) + yl[got].astype(F32)).astype(BF16)
        start(half[i]["zp"])
        start(half[i]["zm"])

    def send_across(i):
        lo, n = PIECES[i]
        pair_rest(lo, n)
        r = DEST[1, 0]
        for slot in range(lo, lo + n):
            value = chip_sum(r, slot)
            value = value + zl[0, leaf_with("zp", slot)].astype(F32)
            value = value + zl[1, leaf_with("zm", slot)].astype(F32)
            sd[r, pl.ds(slot * 128, 128)] = value.astype(BF16)
        start(across[i])

    def send_last(i):
        lo, n = PIECES[i]
        for link, dest, side in (("zp", (0, 1), 0), ("zm", (0, 3), 1)):
            r = DEST[dest]
            for slot in range(lo, lo + n):
                rows = pl.ds(slot * 128, 128)
                value = chip_sum(r, slot)
                got = zh[side, piece_with(link, half, slot)].astype(F32)
                keep = (1 - side) * 128
                sd[r, rows, pl.ds(side * 128, 128)] = (value[:, side * 128:side * 128 + 128] + got).astype(BF16)
                sd[r, rows, pl.ds(keep, 128)] = value[:, keep:keep + 128].astype(BF16)
            start(last[i][link])

    out_copies = []

    def finish(slot):
        q, k = SLOTS[slot]
        rows = pl.ds(slot * 128, 128)
        value = chip_sum(DEST[0, 0], slot)
        value = value + yf[piece_with("y", across, slot)].astype(F32)
        value = value + zf[0, piece_with("zp", last, slot)].astype(F32)
        value = value + zf[1, piece_with("zm", last, slot)].astype(F32)
        out[rows] = value.astype(BF16)
        at = pl.multiple_of(member(q, k, 0) * 64, 128)
        copy = pltpu.make_async_copy(out.at[rows], out_hbm.at[pl.ds(at, 128)], out_sem.at[slot])
        copy.start()
        out_copies.append(copy)

    def both_halves(block):
        arrived(sib[block][0])
        arrived(sib[block][1])

    both_halves((0, 0))
    for copy in w_copies:
        copy.wait()
    dot_in("A")
    arrived(zp0[0])
    start(zp2)
    start(sib[0, 3][0])
    arrived(zm0[1])
    start(zm2)
    start(sib[0, 1][1])
    arrived(y0[0])
    start(zpp[0])
    start(zmp[0])
    start(sib[1, 0][0])
    for copy in d_copies:
        copy.wait()
    dot_out("A", 0, 3)
    start(pairs["A"][0])
    dot_out("A", 3, 8)
    start(pairs["A"][1])
    arrived(zp0[1])
    start(sib[0, 3][1])
    arrived(zm0[0])
    start(sib[0, 1][0])
    arrived(y0[1])
    start(zpp[1])
    start(zmp[1])
    start(sib[1, 0][1])
    send_leaf("A")
    both_halves((0, 1))
    both_halves((0, 3))
    dot_in("B")
    arrived(zp2)
    start(y2[0])
    start(sib[0, 2][0])
    arrived(zm2)
    start(y2[1])
    start(sib[0, 2][1])
    dot_out("B", 0, 3)
    start(pairs["B"][0])
    dot_out("B", 3, 8)
    start(pairs["B"][1])
    both_halves((1, 0))
    both_halves((0, 2))
    dot_in("C")
    send_leaf("B")
    arrived(zpp[0])
    start(sib[1, 3][0])
    arrived(zmp[0])
    start(sib[1, 1][0])
    dot_out("C", 0, 3)
    start(pairs["C"][0])
    dot_out("C", 3, 8)
    start(pairs["C"][1])
    send_leaf("C")
    arrived(zpp[1])
    start(sib[1, 3][1])
    arrived(zmp[1])
    start(sib[1, 1][1])
    both_halves((1, 1))
    both_halves((1, 3))
    dot_in("D")
    arrived(y2[0])
    start(sib[1, 2][0])
    arrived(y2[1])
    start(sib[1, 2][1])
    dot_out("D", 0, 3)
    start(pairs["D"][0])
    send_across(0)
    both_halves((1, 2))
    dot_in("E")
    send_leaf("D")
    dot_out("E", 0, 3)
    start(pairs["E"][0])
    dot_out("D", 3, 8)
    start(pairs["D"][1])
    send_leaf("E")
    dot_out("E", 3, 8)
    start(pairs["E"][1])
    send_half(0)
    send_half(1)
    send_across(1)
    send_half(2)
    send_across(2)
    send_last(0)
    send_last(1)
    send_last(2)
    for slot in range(8):
        finish(slot)
    for copy in started:
        copy.wait_send()
    for copy in out_copies:
        copy.wait()


N_REMOTE = 14 + 16 + 10 + 15 + 15
ANY, VMEM = pl.BlockSpec(memory_space=pl.ANY), pl.BlockSpec(memory_space=pltpu.VMEM)


def on_device(tokens, norm_gain, gate_weight, up_weight, down_weight):
    return pl.pallas_call(
        kernel,
        out_shape=jax.ShapeDtypeStruct((ROWS, COLS), BF16),
        in_specs=[ANY, VMEM, ANY, ANY, ANY],
        out_specs=ANY,
        scratch_shapes=[
            pltpu.VMEM((ROWS, D), BF16),
            pltpu.VMEM((D, 2 * F), BF16),
            pltpu.VMEM((F, D), BF16),
            pltpu.VMEM((128, D), BF16),
            pltpu.VMEM((ROWS, F), BF16),
            pltpu.VMEM((8, ROWS, COLS), F32),
            pltpu.VMEM((8, ROWS, COLS), BF16),
            pltpu.VMEM((8, ROWS, COLS), BF16),
            pltpu.VMEM((7, ROWS, COLS), BF16),
            pltpu.VMEM((ROWS, COLS), BF16),
            pltpu.VMEM((2, ROWS, COLS), BF16),
            pltpu.VMEM((2, ROWS, 128), BF16),
            pltpu.VMEM((ROWS, COLS), BF16),
            pltpu.VMEM((2, ROWS, COLS), BF16),
            pltpu.VMEM((ROWS, COLS), BF16),
            pltpu.SemaphoreType.DMA((31,)),
            pltpu.SemaphoreType.DMA((8,)),
            pltpu.SemaphoreType.REGULAR,
            pltpu.SemaphoreType.DMA((N_REMOTE,)),
            pltpu.SemaphoreType.DMA((N_REMOTE,)),
        ],
        compiler_params=pltpu.CompilerParams(
            collective_id=0, has_side_effects=True, vmem_limit_bytes=67043328),
    )(tokens, norm_gain.reshape(1, D), gate_weight, up_weight, down_weight)


def solution(mesh):
    return jax.shard_map(
        on_device,
        mesh=mesh,
        in_specs=(
            P(("dp", "tensor"), None),
            P(),
            P(None, "tensor"),
            P(None, "tensor"),
            P("tensor", None),
        ),
        out_specs=P("dp", "tensor"),
        check_vma=False,
    )
```

time: 282 us -> 79 us (0.28)
  waiting for transfers between devices: 204 us -> 0 us
  Pallas kernels: 0 us -> 76.9 us
  matrix products: 42.5 us -> 0 us
  blocking collectives: 15 us -> 0 us
  between operations: 13.4 us -> 0.01 us
  other arithmetic: 5.37 us -> 0 us
    reduce_scatter x1 -> x0, waiting for transfers between devices: 129 us -> none  [on_device(): lax.psum_scatter(jnp.einsum('fc,tf->ct', down_weight, hidden, preferred_e...]
    pallas_call x0 -> x1, Pallas kernels: none -> 76.9 us  [on_device(): pl.pallas_call(kernel, out_shape=jax.ShapeDtypeStruct((ROWS, COLS), BF16)...]
    all_gather x1 -> x0, waiting for transfers between devices: 75.4 us -> none  [on_device(): piece = lax.all_gather(normed, 'tensor', axis=0, tiled=True)]
    dot_general x2 -> x0, matrix products: 42.5 us -> none  [the longest x1 27.9 us: on_device(): jnp.einsum('fc,tf->ct', down_weight, hidden, preferred_element_type=jnp.f...]
    all_to_all x1 -> x0, blocking collectives: 15 us -> none  [on_device(): lax.all_to_all(tokens, 'tensor', split_axis=1, concat_axis=0, tiled=True)]
    convert_element_type x2 -> x0, other arithmetic: 4.12 us -> none  [the longest x1 2.13 us: on_device(): return (residual.astype(jnp.float32) + summed.T).astype(jnp.bfloat16)]
  transfers between devices with their start and end apart: 2 -> 0, of which waited for: 2 -> 0; matrix products, arithmetic and copies ran while one was open for 0% -> 0% of each run, Pallas kernels for 0% -> 0%
where the time goes in v1:
time: 79 us; the launch traced here: 78.8 us
  Pallas kernels  76.9 us (97%)
  local copies, waits for them, and re-layouts  1.87 us (2%)
    pallas_call x1, Pallas kernels, on_device(): pl.pallas_call(kernel, out_shape=jax.ShapeDtypeStruct((ROWS, COLS), BF16)...  76.9 us
    unnamed x1, local copies, waits for them, and re-layouts  1.87 us

profile of v1, /device:TPU:0, one launch (start us, length us, event | category | flops | bytes accessed | tf_op | source)
XLA Modules:
  0.0 78.8 jit_solution(10813446363673919789)
XLA Ops:
  0.0 76.9 %shard_map.55 = bf16[1024,256]{1,0:T(8,128)(2,1)} custom-call(bf16[64,4096]{1,0:T(8,128)(2,1)} %tok_hbm.1, f32[1,4096]{1,0:T(1,128)} %bitcast.1, bf16[4096,896]{1,0:T(8,128)(2,1)} %gate_hbm.1, bf16[4096,896]{1,0:T(8,128)(2,1)} %up_hbm.1, bf16[896,4096]{1,0:T(8,128)(2,1)} %down_hbm.1), custom_call_target="tpu_custom_call" | custom-call | tf_op jit(solution)/shard_map/pallas_call | solution.py:354
  76.9 1.9 %copy.7 = bf16[1024,256]{1,0:T(8,128)(2,1)} copy(bf16[1024,256]{1,0:T(8,128)(2,1)} %shard_map.55) | data formatting | bytes 1048576

commit v2 on v0

v2 whole, which is shorter than its diff:
```python
import jax
import jax.numpy as jnp
from jax import lax
from jax.experimental import pallas as pl
from jax.experimental.pallas import tpu as pltpu
from jax.sharding import PartitionSpec as P

MESH = pl.DeviceIdType.MESH
F32, BF16 = jnp.float32, jnp.bfloat16
D, F, ROWS, COLS = 4096, 896, 1024, 256

UNITS = [(0, 0, 0), (0, 0, 1),
         (0, 3, 0), (0, 1, 1), (1, 0, 0),
         (1, 0, 1), (0, 2, 0), (0, 2, 1),
         (0, 3, 1), (0, 1, 0),
         (1, 3, 0), (1, 1, 0), (1, 2, 0), (1, 2, 1),
         (1, 3, 1), (1, 1, 1)]
UNIT = {b: i for i, b in enumerate(UNITS)}
CHUNKS = {"A": (0, 2), "B": (2, 3), "C": (5, 3), "D": (8, 2), "E": (10, 4), "F": (14, 2)}
PIECES = {"AB": (0, 5), "C": (5, 3), "D": (8, 2), "E": (10, 4), "F": (14, 2)}
DESTS = [(1, 2), (1, 1), (1, 3), (0, 2), (1, 0), (0, 1), (0, 3), (0, 0)]
DEST = {b: i for i, b in enumerate(DESTS)}
SEEN = {
    "zp": lambda q, k, h: (q, (k + 1) % 4, h),
    "zm": lambda q, k, h: (q, (k + 3) % 4, h),
    "y": lambda q, k, h: (1 - q, k, h),
}


def kernel(tok_hbm, gain_ref, gate_hbm, up_hbm, down_hbm, out_hbm,
           x, w, dn, res, hid, own, sb, rb, sd, yl, zl, zh, yf, zf, out,
           tok_sem, w_sem, d_sem, out_sem, x_sem, pair_sem, sd_sem, rs):
    dp, t = lax.axis_index("dp"), lax.axis_index("tensor")
    hi, z, c = t // 8, lax.rem(t // 2, 4), lax.rem(t, 2)

    def member(q, k, core):
        return (hi if q == 0 else 1 - hi) * 8 + lax.rem(z + k, 4) * 2 + core

    peer = {
        "zp": (dp, member(0, 1, c)),
        "zm": (dp, member(0, 3, c)),
        "y": (dp, member(1, 0, c)),
        "s": (dp, member(0, 0, 1 - c)),
    }
    barrier = pltpu.get_barrier_semaphore()
    for link in ("y", "zp", "zm", "s"):
        pl.semaphore_signal(barrier, inc=1, device_id=peer[link], device_id_type=MESH)

    tok_copy = pltpu.make_async_copy(tok_hbm, res.at[c], tok_sem)
    tok_copy.start()
    for j in range(7):
        for part, source in enumerate((gate_hbm, up_hbm)):
            pltpu.make_async_copy(
                source.at[:, pl.ds(j * 128, 128)], w.at[:, pl.ds(j * 256 + part * 128, 128)], w_sem).start()

    count = [0]

    def remote(link, source, dst, sem):
        i = count[0]
        count[0] += 1
        return pltpu.make_async_remote_copy(
            src_ref=source, dst_ref=dst, send_sem=sem, recv_sem=rs.at[i],
            device_id=peer[link], device_id_type=MESH)

    def quarter(q, k, i):
        return x.at[UNIT[q, k, i // 2], i % 2, c]

    def gather(link, source, dst):
        return [remote(link, quarter(*source, i), quarter(*dst, i), x_sem) for i in range(4)]

    zp0, zm0, y0 = gather("zp", (0, 0), (0, 3)), gather("zm", (0, 0), (0, 1)), gather("y", (0, 0), (1, 0))
    zp2 = [remote("zp", quarter(0, 3, i), quarter(0, 2, i), x_sem) for i in (0, 1)]
    zm2 = [remote("zm", quarter(0, 1, i), quarter(0, 2, i), x_sem) for i in (3, 2)]
    zpp, zmp, y2 = gather("zp", (1, 0), (1, 3)), gather("zm", (1, 0), (1, 1)), gather("y", (0, 2), (1, 2))
    sib = {u: remote("s", x.at[UNIT[u], :, c], x.at[UNIT[u], :, c], x_sem) for u in UNITS}

    def rows(lo, n):
        return pl.ds(lo * 64, n * 64)

    pairs, leaf = {}, {}
    for name, (lo, n) in CHUNKS.items():
        at = rows(lo, n)
        pairs[name] = [remote("s", sb.at[pl.ds(a, m), at], rb.at[pl.ds(a, m), at], pair_sem) for a, m in ((0, 3), (3, 5))]
        leaf[name] = {
            "y": remote("y", sd.at[DEST[1, 2], at], yl.at[at], sd_sem),
            "zp": remote("zp", sd.at[DEST[1, 1], at], zl.at[0, at], sd_sem),
            "zm": remote("zm", sd.at[DEST[1, 3], at], zl.at[1, at], sd_sem),
        }
    half, across, last = {}, {}, {}
    for name, (lo, n) in PIECES.items():
        at = rows(lo, n)
        half[name] = {
            "zp": remote("zp", sd.at[DEST[0, 2], at, pl.ds(0, 128)], zh.at[0, at], sd_sem),
            "zm": remote("zm", sd.at[DEST[0, 2], at, pl.ds(128, 128)], zh.at[1, at], sd_sem),
        }
        across[name] = {"y": remote("y", sd.at[DEST[1, 0], at], yf.at[at], sd_sem)}
        last[name] = {
            "zp": remote("zp", sd.at[DEST[0, 1], at], zf.at[0, at], sd_sem),
            "zm": remote("zm", sd.at[DEST[0, 3], at], zf.at[1, at], sd_sem),
        }

    waited = set()

    def arrived(copy):
        if id(copy) not in waited:
            waited.add(id(copy))
            copy.wait_recv()

    def seen(messages, link, unit, table):
        s = UNIT[SEEN[link](*UNITS[unit])]
        for name, (lo, n) in table.items():
            if lo <= s < lo + n:
                arrived(messages[name][link])
        return rows(s, 1)

    res[1 - c] = jnp.zeros((4, 16, D), BF16)
    tok_copy.wait()
    gain = gain_ref[...]
    for i in range(4):
        wide = res[c, i].astype(F32)
        square_mean = jnp.mean(wide * wide, axis=1, keepdims=True)
        normed = wide * gain / jnp.sqrt(square_mean + 1e-05)
        x[i // 2, i % 2, c] = normed.astype(BF16)
    pl.semaphore_wait(barrier, 4)

    sib[0, 0, 0].start()
    sib[0, 0, 1].start()
    for i in range(3):
        zp0[i].start()
        zm0[3 - i].start()
        y0[i].start()
    y0[3].start()
    for r, (q, k) in enumerate(DESTS):
        for part, core in enumerate((1 - c, c)):
            col = pl.multiple_of(member(q, k, core) * COLS, COLS)
            pltpu.make_async_copy(
                down_hbm.at[:, pl.ds(col, COLS)], dn.at[:, pl.ds((2 * r + part) * COLS, COLS)], d_sem).start()

    def dot_in(lo, n):
        both = jnp.dot(x[pl.ds(lo, n)].reshape(n * 64, D), w[...], preferred_element_type=F32)
        for j in range(7):
            gate, up = both[:, j * 256:j * 256 + 128], both[:, j * 256 + 128:j * 256 + 256]
            hid[rows(lo, n), pl.ds(j * 128, 128)] = (gate / (1.0 + jnp.exp(-gate)) * up).astype(BF16)

    def dot_out(lo, n, first, end):
        part = jnp.dot(hid[rows(lo, n)], dn[:, pl.ds(first * 512, (end - first) * 512)], preferred_element_type=F32)
        for r in range(first, end):
            for side in range(2):
                at = (r - first) * 512 + side * 256
                value = part[:, at:at + 256]
                if lo == 0:
                    core = (1 - c, c)[side]
                    col = pl.multiple_of(member(*DESTS[r], core) * COLS, COLS)
                    add = [res[kk, i, :, pl.ds(col, COLS)].astype(F32) for i in range(4) for kk in range(2)]
                    value = value + jnp.concatenate(add, axis=0)
                if side == 0:
                    sb[r, rows(lo, n)] = value.astype(BF16)
                else:
                    own[r, rows(lo, n)] = value

    def chip_sum(r, unit):
        return own[r, rows(unit, 1)] + rb[r, rows(unit, 1)].astype(F32)

    def send_leaf(name, links=("y", "zp", "zm")):
        lo, n = CHUNKS[name]
        arrived(pairs[name][0])
        for link in links:
            r = DEST[{"y": (1, 2), "zp": (1, 1), "zm": (1, 3)}[link]]
            for unit in range(lo, lo + n):
                sd[r, rows(unit, 1)] = chip_sum(r, unit).astype(BF16)
            leaf[name][link].start()

    def pair_rest(lo, n):
        for name, (a, m) in CHUNKS.items():
            if a < lo + n and lo < a + m:
                arrived(pairs[name][1])

    def send_half(name):
        lo, n = PIECES[name]
        pair_rest(lo, n)
        r = DEST[0, 2]
        for unit in range(lo, lo + n):
            got = seen(leaf, "y", unit, CHUNKS)
            sd[r, rows(unit, 1)] = (chip_sum(r, unit) + yl[got].astype(F32)).astype(BF16)
        half[name]["zp"].start()
        half[name]["zm"].start()

    def send_across(name):
        lo, n = PIECES[name]
        pair_rest(lo, n)
        r = DEST[1, 0]
        for unit in range(lo, lo + n):
            value = chip_sum(r, unit)
            value = value + zl[0, seen(leaf, "zp", unit, CHUNKS)].astype(F32)
            value = value + zl[1, seen(leaf, "zm", unit, CHUNKS)].astype(F32)
            sd[r, rows(unit, 1)] = value.astype(BF16)
        across[name]["y"].start()

    def send_last(name):
        lo, n = PIECES[name]
        for link, dest, side in (("zp", (0, 1), 0), ("zm", (0, 3), 1)):
            r = DEST[dest]
            for unit in range(lo, lo + n):
                value = chip_sum(r, unit)
                got = zh[side, seen(half, link, unit, PIECES)].astype(F32)
                keep = (1 - side) * 128
                sd[r, rows(unit, 1), pl.ds(side * 128, 128)] = (value[:, side * 128:side * 128 + 128] + got).astype(BF16)
                sd[r, rows(unit, 1), pl.ds(keep, 128)] = value[:, keep:keep + 128].astype(BF16)
            last[name][link].start()

    out_copies = []

    def finish(unit):
        q, k, h = UNITS[unit]
        value = chip_sum(DEST[0, 0], unit)
        value = value + yf[seen(across, "y", unit, PIECES)].astype(F32)
        value = value + zf[0, seen(last, "zp", unit, PIECES)].astype(F32)
        value = value + zf[1, seen(last, "zm", unit, PIECES)].astype(F32)
        ordered = [value[i * 32 + core * 16:i * 32 + core * 16 + 16] for core in range(2) for i in range(2)]
        out[rows(unit, 1)] = jnp.concatenate(ordered, axis=0).astype(BF16)
        for core in range(2):
            at = pl.multiple_of(member(q, k, core) * 64 + h * 32, 32)
            copy = pltpu.make_async_copy(
                out.at[pl.ds(unit * 64 + core * 32, 32)], out_hbm.at[pl.ds(at, 32)], out_sem)
            copy.start()
            out_copies.append(copy)

    def exchange(*units):
        for unit in units:
            sib[unit].start()

    def have(*units):
        for unit in units:
            arrived(sib[unit])

    def all_sent(ref, sem):
        pltpu.make_async_remote_copy(
            src_ref=ref, dst_ref=ref, send_sem=sem, recv_sem=rs.at[0],
            device_id=peer["s"], device_id_type=MESH).wait_send()

    have((0, 0, 0), (0, 0, 1))
    pltpu.make_async_copy(w, w, w_sem).wait()
    dot_in(0, 2)
    arrived(zp0[0])
    zp2[0].start()
    arrived(zm0[3])
    zm2[0].start()
    pltpu.make_async_copy(dn, dn, d_sem).wait()
    dot_out(0, 2, 0, 3)
    pairs["A"][0].start()
    dot_out(0, 2, 3, 8)
    pairs["A"][1].start()
    arrived(zp0[1])
    zp2[1].start()
    zp0[3].start()
    exchange((0, 3, 0))
    arrived(zm0[2])
    zm2[1].start()
    zm0[0].start()
    exchange((0, 1, 1))
    for i in range(2):
        arrived(y0[i])
        zpp[i].start()
        zmp[i].start()
    exchange((1, 0, 0))
    have((0, 3, 0), (0, 1, 1), (1, 0, 0))
    dot_in(2, 3)
    send_leaf("A", ("y",))
    dot_out(2, 3, 0, 3)
    pairs["B"][0].start()
    for i in range(2, 4):
        arrived(y0[i])
        zpp[i].start()
        zmp[i].start()
    exchange((1, 0, 1))
    arrived(zp2[0])
    y2[0].start()
    arrived(zm2[0])
    y2[3].start()
    dot_out(2, 3, 3, 8)
    pairs["B"][1].start()
    send_leaf("A", ("zp", "zm"))
    arrived(zp2[1])
    y2[1].start()
    exchange((0, 2, 0))
    arrived(zm2[1])
    y2[2].start()
    exchange((0, 2, 1))
    send_leaf("B")
    have((1, 0, 1), (0, 2, 0), (0, 2, 1))
    dot_in(5, 3)
    arrived(zp0[2])
    arrived(zp0[3])
    exchange((0, 3, 1))
    arrived(zm0[1])
    arrived(zm0[0])
    exchange((0, 1, 0))
    dot_out(5, 3, 0, 3)
    pairs["C"][0].start()
    dot_out(5, 3, 3, 8)
    pairs["C"][1].start()
    have((0, 3, 1), (0, 1, 0))
    dot_in(8, 2)
    send_leaf("C")
    for copies, unit in ((zpp, (1, 3, 0)), (zmp, (1, 1, 0))):
        arrived(copies[0])
        arrived(copies[1])
        exchange(unit)
    dot_out(8, 2, 0, 3)
    pairs["D"][0].start()
    dot_out(8, 2, 3, 8)
    pairs["D"][1].start()
    have((1, 3, 0), (1, 1, 0))
    dot_in(10, 2)
    send_leaf("D")
    for h in range(2):
        arrived(y2[2 * h])
        arrived(y2[2 * h + 1])
        exchange((1, 2, h))
    have((1, 2, 0), (1, 2, 1))
    dot_in(12, 2)
    for copies, unit in ((zpp, (1, 3, 1)), (zmp, (1, 1, 1))):
        arrived(copies[2])
        arrived(copies[3])
        exchange(unit)
    dot_out(10, 4, 0, 3)
    pairs["E"][0].start()
    have((1, 3, 1), (1, 1, 1))
    dot_in(14, 2)
    send_leaf("E")
    dot_out(14, 2, 0, 3)
    pairs["F"][0].start()
    dot_out(10, 4, 3, 8)
    pairs["E"][1].start()
    send_leaf("F")
    dot_out(14, 2, 3, 8)
    pairs["F"][1].start()
    send_half("C")
    send_half("E")
    send_across("D")
    send_half("AB")
    send_half("D")
    send_half("F")
    send_across("AB")
    send_across("F")
    send_across("E")
    send_across("C")
    for name in ("F", "D", "AB", "E", "C"):
        send_last(name)
    for name in ("F", "D", "AB", "E", "C"):
        lo, n = PIECES[name]
        for unit in range(lo, lo + n):
            finish(unit)
    all_sent(x.at[pl.ds(0, 15)], x_sem)
    all_sent(sb, pair_sem)
    all_sent(sd, sd_sem)
    pltpu.make_async_copy(out, out_hbm, out_sem).wait()


N_REMOTE = 28 + 16 + 6 * 5 + 5 * 5
ANY, VMEM = pl.BlockSpec(memory_space=pl.ANY), pl.BlockSpec(memory_space=pltpu.VMEM)


def on_device(tokens, norm_gain, gate_weight, up_weight, down_weight):
    return pl.pallas_call(
        kernel,
        out_shape=jax.ShapeDtypeStruct((ROWS, COLS), BF16),
        in_specs=[ANY, VMEM, ANY, ANY, ANY],
        out_specs=ANY,
        scratch_shapes=[
            pltpu.VMEM((16, 2, 2, 16, D), BF16),
            pltpu.VMEM((D, 2 * F), BF16),
            pltpu.VMEM((F, D), BF16),
            pltpu.VMEM((2, 4, 16, D), BF16),
            pltpu.VMEM((ROWS, F), BF16),
            pltpu.VMEM((8, ROWS, COLS), F32),
            pltpu.VMEM((8, ROWS, COLS), BF16),
            pltpu.VMEM((8, ROWS, COLS), BF16),
            pltpu.VMEM((7, ROWS, COLS), BF16),
            pltpu.VMEM((ROWS, COLS), BF16),
            pltpu.VMEM((2, ROWS, COLS), BF16),
            pltpu.VMEM((2, ROWS, 128), BF16),
            pltpu.VMEM((ROWS, COLS), BF16),
            pltpu.VMEM((2, ROWS, COLS), BF16),
            pltpu.VMEM((ROWS, COLS), BF16),
            pltpu.SemaphoreType.DMA,
            pltpu.SemaphoreType.DMA,
            pltpu.SemaphoreType.DMA,
            pltpu.SemaphoreType.DMA,
            pltpu.SemaphoreType.DMA,
            pltpu.SemaphoreType.DMA,
            pltpu.SemaphoreType.DMA,
            pltpu.SemaphoreType.DMA((N_REMOTE,)),
        ],
        compiler_params=pltpu.CompilerParams(
            collective_id=0, has_side_effects=True, vmem_limit_bytes=67043328),
    )(tokens.reshape(4, 16, D), norm_gain.reshape(1, D), gate_weight, up_weight, down_weight)


def solution(mesh):
    return jax.shard_map(
        on_device,
        mesh=mesh,
        in_specs=(
            P(("dp", "tensor"), None),
            P(),
            P(None, "tensor"),
            P(None, "tensor"),
            P("tensor", None),
        ),
        out_specs=P("dp", "tensor"),
        check_vma=False,
    )
```

time: 282 us -> 76.7 us (0.27)
  waiting for transfers between devices: 204 us -> 0 us
  Pallas kernels: 0 us -> 74.7 us
  matrix products: 42.5 us -> 0 us
  blocking collectives: 15 us -> 0 us
  between operations: 13.4 us -> 0.01 us
  other arithmetic: 5.37 us -> 0 us
    reduce_scatter x1 -> x0, waiting for transfers between devices: 129 us -> none  [on_device(): lax.psum_scatter(jnp.einsum('fc,tf->ct', down_weight, hidden, preferred_e...]
    all_gather x1 -> x0, waiting for transfers between devices: 75.4 us -> none  [on_device(): piece = lax.all_gather(normed, 'tensor', axis=0, tiled=True)]
    pallas_call x0 -> x1, Pallas kernels: none -> 74.7 us  [on_device(): pl.pallas_call(kernel, out_shape=jax.ShapeDtypeStruct((ROWS, COLS), BF16)...]
    dot_general x2 -> x0, matrix products: 42.5 us -> none  [the longest x1 27.9 us: on_device(): jnp.einsum('fc,tf->ct', down_weight, hidden, preferred_element_type=jnp.f...]
    all_to_all x1 -> x0, blocking collectives: 15 us -> none  [on_device(): lax.all_to_all(tokens, 'tensor', split_axis=1, concat_axis=0, tiled=True)]
    convert_element_type x2 -> x0, other arithmetic: 4.12 us -> none  [the longest x1 2.13 us: on_device(): return (residual.astype(jnp.float32) + summed.T).astype(jnp.bfloat16)]
  transfers between devices with their start and end apart: 2 -> 0, of which waited for: 2 -> 0; matrix products, arithmetic and copies ran while one was open for 0% -> 0% of each run, Pallas kernels for 0% -> 0%
where the time goes in v2:
time: 76.7 us; the launch traced here: 76.5 us
  Pallas kernels  74.7 us (97%)
  local copies, waits for them, and re-layouts  1.87 us (2%)
    pallas_call x1, Pallas kernels, on_device(): pl.pallas_call(kernel, out_shape=jax.ShapeDtypeStruct((ROWS, COLS), BF16)...  74.7 us
    unnamed x1, local copies, waits for them, and re-layouts  1.87 us

profile of v2, /device:TPU:0, one launch (start us, length us, event | category | flops | bytes accessed | tf_op | source)
XLA Modules:
  0.0 76.5 jit_solution(4057081141715408570)
XLA Ops:
  0.0 74.7 %shard_map.55 = bf16[1024,256]{1,0:T(8,128)(2,1)} custom-call(bf16[4,16,4096]{2,1,0:T(8,128)(2,1)} %bitcast.2, f32[1,4096]{1,0:T(1,128)} %bitcast.3, bf16[4096,896]{1,0:T(8,128)(2,1)} %gate_hbm.1, bf16[4096,896]{1,0:T(8,128)(2,1)} %up_hbm.1, bf16[896,4096]{1,0:T(8,128)(2,1)} %down_hbm.1), custom_call_target="tpu_custom_call" | custom-call | tf_op jit(solution)/shard_map/pallas_call | solution.py:365
  74.7 1.9 %copy.7 = bf16[1024,256]{1,0:T(8,128)(2,1)} copy(bf16[1024,256]{1,0:T(8,128)(2,1)} %shard_map.55) | data formatting | bytes 1048576

commit v3 on v2

--- a/solution.py
+++ b/solution.py
@@ -16,10 +16,18 @@
          (1, 3, 0), (1, 1, 0), (1, 2, 0), (1, 2, 1),
          (1, 3, 1), (1, 1, 1)]
 UNIT = {b: i for i, b in enumerate(UNITS)}
+QUARTERED = [(0, 3, 0), (0, 1, 1), (1, 0, 0), (1, 3, 1), (1, 1, 1)]
 CHUNKS = {"A": (0, 2), "B": (2, 3), "C": (5, 3), "D": (8, 2), "E": (10, 4), "F": (14, 2)}
-PIECES = {"AB": (0, 5), "C": (5, 3), "D": (8, 2), "E": (10, 4), "F": (14, 2)}
 DESTS = [(1, 2), (1, 1), (1, 3), (0, 2), (1, 0), (0, 1), (0, 3), (0, 0)]
 DEST = {b: i for i, b in enumerate(DESTS)}
+HALF = [[(0, 0, 0), (0, 0, 1), (1, 0, 0), (1, 0, 1)],
+        [(1, 2, 0), (1, 2, 1), (1, 3, 0), (1, 1, 0), (0, 2, 0), (0, 2, 1), (0, 3, 0), (0, 1, 0)],
+        [(0, 3, 1), (0, 1, 1), (1, 3, 1), (1, 1, 1)]]
+ACROSS = [[(0, k, h) for k in range(4) for h in range(2)], [(1, k, 0) for k in range(4)], [(1, k, 1) for k in range(4)]]
+LAST = {link: [[(0, p, 0), (0, p, 1)],
+               [(1, p, 0), (0, m, 0), (0, m, 1), (1, 2, 0), (1, m, 0), (0, 0, 0), (0, 2, 0), (1, 0, 0)],
+               [(1, p, 1), (1, m, 1), (0, 0, 1), (0, 2, 1), (1, 0, 1), (1, 2, 1)]]
+        for link, p, m in (("zp", 3, 1), ("zm", 1, 3))}
 SEEN = {
     "zp": lambda q, k, h: (q, (k + 1) % 4, h),
     "zm": lambda q, k, h: (q, (k + 3) % 4, h),
@@ -27,9 +35,9 @@
 }
 
 
-def kernel(tok_hbm, gain_ref, gate_hbm, up_hbm, down_hbm, out_hbm,
-           x, w, dn, res, hid, own, sb, rb, sd, yl, zl, zh, yf, zf, out,
-           tok_sem, w_sem, d_sem, out_sem, x_sem, pair_sem, sd_sem, rs):
+def kernel(tok_hbm, gain_ref, gate_hbm, up_hbm, down_hbm, out,
+           x, w, dn, res, hid, own, sb, rb, sd, yl, zl, zh, yf, zf,
+           tok_sem, w_sem, d_sem, x_sem, pair_sem, sd_sem, rs):
     dp, t = lax.axis_index("dp"), lax.axis_index("tensor")
     hi, z, c = t // 8, lax.rem(t // 2, 4), lax.rem(t, 2)
 
@@ -48,11 +56,6 @@
 
     tok_copy = pltpu.make_async_copy(tok_hbm, res.at[c], tok_sem)
     tok_copy.start()
-    for j in range(7):
-        for part, source in enumerate((gate_hbm, up_hbm)):
-            pltpu.make_async_copy(
-                source.at[:, pl.ds(j * 128, 128)], w.at[:, pl.ds(j * 256 + part * 128, 128)], w_sem).start()
-
     count = [0]
 
     def remote(link, source, dst, sem):
@@ -72,7 +75,12 @@
     zp2 = [remote("zp", quarter(0, 3, i), quarter(0, 2, i), x_sem) for i in (0, 1)]
     zm2 = [remote("zm", quarter(0, 1, i), quarter(0, 2, i), x_sem) for i in (3, 2)]
     zpp, zmp, y2 = gather("zp", (1, 0), (1, 3)), gather("zm", (1, 0), (1, 1)), gather("y", (0, 2), (1, 2))
-    sib = {u: remote("s", x.at[UNIT[u], :, c], x.at[UNIT[u], :, c], x_sem) for u in UNITS}
+    sib = {}
+    for u in UNITS:
+        if u in QUARTERED:
+            sib[u] = [remote("s", x.at[UNIT[u], i, c], x.at[UNIT[u], i, c], x_sem) for i in range(2)]
+        else:
+            sib[u] = [remote("s", x.at[UNIT[u], :, c], x.at[UNIT[u], :, c], x_sem)]
 
     def rows(lo, n):
         return pl.ds(lo * 64, n * 64)
@@ -86,18 +94,23 @@
             "zp": remote("zp", sd.at[DEST[1, 1], at], zl.at[0, at], sd_sem),
             "zm": remote("zm", sd.at[DEST[1, 3], at], zl.at[1, at], sd_sem),
         }
-    half, across, last = {}, {}, {}
-    for name, (lo, n) in PIECES.items():
-        at = rows(lo, n)
-        half[name] = {
-            "zp": remote("zp", sd.at[DEST[0, 2], at, pl.ds(0, 128)], zh.at[0, at], sd_sem),
-            "zm": remote("zm", sd.at[DEST[0, 2], at, pl.ds(128, 128)], zh.at[1, at], sd_sem),
-        }
-        across[name] = {"y": remote("y", sd.at[DEST[1, 0], at], yf.at[at], sd_sem)}
-        last[name] = {
-            "zp": remote("zp", sd.at[DEST[0, 1], at], zf.at[0, at], sd_sem),
-            "zm": remote("zm", sd.at[DEST[0, 3], at], zf.at[1, at], sd_sem),
-        }
+    def pieces(orders, make):
+        copies, where, at = [], {}, 0
+        for i, units in enumerate(orders):
+            copies.append(make(rows(at, len(units))))
+            for unit in units:
+                where[unit] = (i, at)
+                at += 1
+        return copies, where
+
+    half = {}
+    for link, side in (("zp", 0), ("zm", 1)):
+        half[link] = pieces(HALF, lambda at: remote(
+            link, sd.at[DEST[0, 2], at, pl.ds(side * 128, 128)], zh.at[side, at], sd_sem))
+    across = {"y": pieces(ACROSS, lambda at: remote("y", sd.at[DEST[1, 0], at], yf.at[at], sd_sem))}
+    last = {}
+    for link, side, k in (("zp", 0, 1), ("zm", 1, 3)):
+        last[link] = pieces(LAST[link], lambda at: remote(link, sd.at[DEST[0, k], at], zf.at[side, at], sd_sem))
 
     waited = set()
 
@@ -106,15 +119,30 @@
             waited.add(id(copy))
             copy.wait_recv()
 
-    def seen(messages, link, unit, table):
-        s = UNIT[SEEN[link](*UNITS[unit])]
-        for name, (lo, n) in table.items():
-            if lo <= s < lo + n:
-                arrived(messages[name][link])
-        return rows(s, 1)
+    def seen_leaf(link, unit):
+        at = UNIT[SEEN[link](*unit)]
+        for name, (lo, n) in CHUNKS.items():
+            if lo <= at < lo + n:
+                arrived(leaf[name][link])
+        return rows(at, 1)
+
+    def seen(messages, link, unit):
+        copies, where = messages[link]
+        i, at = where[SEEN[link](*unit)]
+        arrived(copies[i])
+        return rows(at, 1)
+
+    def exchange(*units):
+        for unit in units:
+            for copy in sib[unit]:
+                copy.start()
 
     res[1 - c] = jnp.zeros((4, 16, D), BF16)
     tok_copy.wait()
+    for j in range(7):
+        for part, source in enumerate((gate_hbm, up_hbm)):
+            pltpu.make_async_copy(
+                source.at[:, pl.ds(j * 128, 128)], w.at[:, pl.ds(j * 256 + part * 128, 128)], w_sem).start()
     gain = gain_ref[...]
     for i in range(4):
         wide = res[c, i].astype(F32)
@@ -123,8 +151,7 @@
         x[i // 2, i % 2, c] = normed.astype(BF16)
     pl.semaphore_wait(barrier, 4)
 
-    sib[0, 0, 0].start()
-    sib[0, 0, 1].start()
+    exchange((0, 0, 0), (0, 0, 1))
     for i in range(3):
         zp0[i].start()
         zm0[3 - i].start()
@@ -158,80 +185,68 @@
                 else:
                     own[r, rows(lo, n)] = value
 
-    def chip_sum(r, unit):
-        return own[r, rows(unit, 1)] + rb[r, rows(unit, 1)].astype(F32)
+    def chip_sum(r, unit, rest=True):
+        at = UNIT[unit]
+        for name, (lo, n) in CHUNKS.items():
+            if lo <= at < lo + n:
+                arrived(pairs[name][1 if rest else 0])
+        return own[r, rows(at, 1)] + rb[r, rows(at, 1)].astype(F32)
 
     def send_leaf(name, links=("y", "zp", "zm")):
         lo, n = CHUNKS[name]
-        arrived(pairs[name][0])
         for link in links:
             r = DEST[{"y": (1, 2), "zp": (1, 1), "zm": (1, 3)}[link]]
             for unit in range(lo, lo + n):
-                sd[r, rows(unit, 1)] = chip_sum(r, unit).astype(BF16)
+                sd[r, rows(unit, 1)] = chip_sum(r, UNITS[unit], False).astype(BF16)
             leaf[name][link].start()
 
-    def pair_rest(lo, n):
-        for name, (a, m) in CHUNKS.items():
-            if a < lo + n and lo < a + m:
-                arrived(pairs[name][1])
-
-    def send_half(name):
-        lo, n = PIECES[name]
-        pair_rest(lo, n)
+    def send_half(i):
         r = DEST[0, 2]
-        for unit in range(lo, lo + n):
-            got = seen(leaf, "y", unit, CHUNKS)
-            sd[r, rows(unit, 1)] = (chip_sum(r, unit) + yl[got].astype(F32)).astype(BF16)
-        half[name]["zp"].start()
-        half[name]["zm"].start()
-
-    def send_across(name):
-        lo, n = PIECES[name]
-        pair_rest(lo, n)
+        where = half["zp"][1]
+        for unit in HALF[i]:
+            got = seen_leaf("y", unit)
+            sd[r, rows(where[unit][1], 1)] = (chip_sum(r, unit) + yl[got].astype(F32)).astype(BF16)
+        half["zp"][0][i].start()
+        half["zm"][0][i].start()
+
+    def send_across(i):
         r = DEST[1, 0]
-        for unit in range(lo, lo + n):
+        copies, where = across["y"]
+        for unit in ACROSS[i]:
             value = chip_sum(r, unit)
-            value = value + zl[0, seen(leaf, "zp", unit, CHUNKS)].astype(F32)
-            value = value + zl[1, seen(leaf, "zm", unit, CHUNKS)].astype(F32)
-            sd[r, rows(unit, 1)] = value.astype(BF16)
-        across[name]["y"].start()
-
-    def send_last(name):
-        lo, n = PIECES[name]
-        for link, dest, side in (("zp", (0, 1), 0), ("zm", (0, 3), 1)):
-            r = DEST[dest]
-            for unit in range(lo, lo + n):
+            value = value + zl[0, seen_leaf("zp", unit)].astype(F32)
+            value = value + zl[1, seen_leaf("zm", unit)].astype(F32)
+            sd[r, rows(where[unit][1], 1)] = value.astype(BF16)
+        copies[i].start()
+
+    def send_last(i):
+        for link, side, k in (("zp", 0, 1), ("zm", 1, 3)):
+            r = DEST[0, k]
+            copies, where = last[link]
+            for unit in LAST[link][i]:
                 value = chip_sum(r, unit)
-                got = zh[side, seen(half, link, unit, PIECES)].astype(F32)
+                got = zh[side, seen(half, link, unit)].astype(F32)
                 keep = (1 - side) * 128
-                sd[r, rows(unit, 1), pl.ds(side * 128, 128)] = (value[:, side * 128:side * 128 + 128] + got).astype(BF16)
-                sd[r, rows(unit, 1), pl.ds(keep, 128)] = value[:, keep:keep + 128].astype(BF16)
-            last[name][link].start()
-
-    out_copies = []
+                at = rows(where[unit][1], 1)
+                sd[r, at, pl.ds(side * 128, 128)] = (value[:, side * 128:side * 128 + 128] + got).astype(BF16)
+                sd[r, at, pl.ds(keep, 128)] = value[:, keep:keep + 128].astype(BF16)
+            copies[i].start()
 
     def finish(unit):
-        q, k, h = UNITS[unit]
+        q, k, h = unit
         value = chip_sum(DEST[0, 0], unit)
-        value = value + yf[seen(across, "y", unit, PIECES)].astype(F32)
-        value = value + zf[0, seen(last, "zp", unit, PIECES)].astype(F32)
-        value = value + zf[1, seen(last, "zm", unit, PIECES)].astype(F32)
-        ordered = [value[i * 32 + core * 16:i * 32 + core * 16 + 16] for core in range(2) for i in range(2)]
-        out[rows(unit, 1)] = jnp.concatenate(ordered, axis=0).astype(BF16)
+        value = value + yf[seen(across, "y", unit)].astype(F32)
+        value = value + zf[0, seen(last, "zp", unit)].astype(F32)
+        value = value + zf[1, seen(last, "zm", unit)].astype(F32)
         for core in range(2):
             at = pl.multiple_of(member(q, k, core) * 64 + h * 32, 32)
-            copy = pltpu.make_async_copy(
-                out.at[pl.ds(unit * 64 + core * 32, 32)], out_hbm.at[pl.ds(at, 32)], out_sem)
-            copy.start()
-            out_copies.append(copy)
-
-    def exchange(*units):
-        for unit in units:
-            sib[unit].start()
+            ordered = [value[i * 32 + core * 16:i * 32 + core * 16 + 16] for i in range(2)]
+            out[pl.ds(at, 32)] = jnp.concatenate(ordered, axis=0).astype(BF16)
 
     def have(*units):
         for unit in units:
-            arrived(sib[unit])
+            for copy in sib[unit]:
+                arrived(copy)
 
     def all_sent(ref, sem):
         pltpu.make_async_remote_copy(
@@ -243,8 +258,12 @@
     dot_in(0, 2)
     arrived(zp0[0])
     zp2[0].start()
+    sib[0, 3, 0][0].start()
     arrived(zm0[3])
     zm2[0].start()
+    sib[0, 1, 1][1].start()
+    arrived(y0[0])
+    sib[1, 0, 0][0].start()
     pltpu.make_async_copy(dn, dn, d_sem).wait()
     dot_out(0, 2, 0, 3)
     pairs["A"][0].start()
@@ -253,16 +272,16 @@
     arrived(zp0[1])
     zp2[1].start()
     zp0[3].start()
-    exchange((0, 3, 0))
+    sib[0, 3, 0][1].start()
     arrived(zm0[2])
     zm2[1].start()
     zm0[0].start()
-    exchange((0, 1, 1))
+    sib[0, 1, 1][0].start()
+    arrived(y0[1])
+    sib[1, 0, 0][1].start()
     for i in range(2):
-        arrived(y0[i])
         zpp[i].start()
         zmp[i].start()
-    exchange((1, 0, 0))
     have((0, 3, 0), (0, 1, 1), (1, 0, 0))
     dot_in(2, 3)
     send_leaf("A", ("y",))
@@ -319,54 +338,49 @@
         exchange((1, 2, h))
     have((1, 2, 0), (1, 2, 1))
     dot_in(12, 2)
-    for copies, unit in ((zpp, (1, 3, 1)), (zmp, (1, 1, 1))):
-        arrived(copies[2])
-        arrived(copies[3])
-        exchange(unit)
+    for i in (2, 3):
+        for copies, unit in ((zpp, (1, 3, 1)), (zmp, (1, 1, 1))):
+            arrived(copies[i])
+            sib[unit][i - 2].start()
     dot_out(10, 4, 0, 3)
     pairs["E"][0].start()
+    send_half(0)
+    dot_out(10, 4, 3, 8)
+    pairs["E"][1].start()
+    send_leaf("E")
+    send_across(0)
     have((1, 3, 1), (1, 1, 1))
     dot_in(14, 2)
-    send_leaf("E")
+    send_last(0)
     dot_out(14, 2, 0, 3)
     pairs["F"][0].start()
-    dot_out(10, 4, 3, 8)
-    pairs["E"][1].start()
-    send_leaf("F")
+    send_half(1)
     dot_out(14, 2, 3, 8)
     pairs["F"][1].start()
-    send_half("C")
-    send_half("E")
-    send_across("D")
-    send_half("AB")
-    send_half("D")
-    send_half("F")
-    send_across("AB")
-    send_across("F")
-    send_across("E")
-    send_across("C")
-    for name in ("F", "D", "AB", "E", "C"):
-        send_last(name)
-    for name in ("F", "D", "AB", "E", "C"):
-        lo, n = PIECES[name]
-        for unit in range(lo, lo + n):
-            finish(unit)
+    send_leaf("F")
+    send_across(1)
+    send_last(1)
+    send_half(2)
+    send_across(2)
+    send_last(2)
+    piece = {u: max(last[link][1][SEEN[link](*u)][0] for link in ("zp", "zm")) for u in UNITS}
+    for unit in sorted(UNITS, key=lambda u: piece[u]):
+        finish(unit)
     all_sent(x.at[pl.ds(0, 15)], x_sem)
     all_sent(sb, pair_sem)
     all_sent(sd, sd_sem)
-    pltpu.make_async_copy(out, out_hbm, out_sem).wait()
-
-
-N_REMOTE = 28 + 16 + 6 * 5 + 5 * 5
+
+
+N_REMOTE = 28 + 16 + 5 + 6 * 5 + 15
 ANY, VMEM = pl.BlockSpec(memory_space=pl.ANY), pl.BlockSpec(memory_space=pltpu.VMEM)
 
 
 def on_device(tokens, norm_gain, gate_weight, up_weight, down_weight):
     return pl.pallas_call(
         kernel,
-        out_shape=jax.ShapeDtypeStruct((ROWS, COLS), BF16),
+        out_shape=pltpu.VMEM((ROWS, COLS), BF16),
         in_specs=[ANY, VMEM, ANY, ANY, ANY],
-        out_specs=ANY,
+        out_specs=VMEM,
         scratch_shapes=[
             pltpu.VMEM((16, 2, 2, 16, D), BF16),
             pltpu.VMEM((D, 2 * F), BF16),
@@ -382,8 +396,6 @@
             pltpu.VMEM((2, ROWS, 128), BF16),
             pltpu.VMEM((ROWS, COLS), BF16),
             pltpu.VMEM((2, ROWS, COLS), BF16),
-            pltpu.VMEM((ROWS, COLS), BF16),
-            pltpu.SemaphoreType.DMA,
             pltpu.SemaphoreType.DMA,
             pltpu.SemaphoreType.DMA,
             pltpu.SemaphoreType.DMA,
@@ -393,7 +405,7 @@
             pltpu.SemaphoreType.DMA((N_REMOTE,)),
         ],
         compiler_params=pltpu.CompilerParams(
-            collective_id=0, has_side_effects=True, vmem_limit_bytes=67043328),
+            collective_id=0, has_side_effects=True, vmem_limit_bytes=62 * 2**20),
     )(tokens.reshape(4, 16, D), norm_gain.reshape(1, D), gate_weight, up_weight, down_weight)
 
 

time: 76.7 us -> 69.5 us (0.906)
  Pallas kernels: 74.7 us -> 68.1 us
  local copies, waits for them, and re-layouts: 1.87 us -> 0.8 us
    pallas_call x1, Pallas kernels: 74.7 us -> 68.1 us  [on_device(): pl.pallas_call(kernel, out_shape=pltpu.VMEM((ROWS, COLS), BF16), in_specs...]
    unnamed x1, local copies, waits for them, and re-layouts: 1.87 us -> 0.8 us
where the time goes in v3:
time: 69.5 us; the launch traced here: 68.9 us
  Pallas kernels  68.1 us (98%)
  local copies, waits for them, and re-layouts  0.8 us (1%)
    pallas_call x1, Pallas kernels, on_device(): pl.pallas_call(kernel, out_shape=pltpu.VMEM((ROWS, COLS), BF16), in_specs...  68.1 us

profile of v3, /device:TPU:0, one launch (start us, length us, event | category | flops | bytes accessed | tf_op | source)
XLA Modules:
  0.0 68.9 jit_solution(14319322022750325055)
XLA Ops:
  0.0 68.1 %shard_map.55 = bf16[1024,256]{1,0:T(8,128)(2,1)S(1)} custom-call(bf16[4,16,4096]{2,1,0:T(8,128)(2,1)} %bitcast.2, f32[1,4096]{1,0:T(1,128)} %bitcast.3, bf16[4096,896]{1,0:T(8,128)(2,1)} %gate_hbm.1, bf16[4096,896]{1,0:T(8,128)(2,1)} %up_hbm.1, bf16[896,4096]{1,0:T(8,128)(2,1)} %down_hbm.1), custom_call_target="tpu_custom_call" | custom-call | tf_op jit(solution)/shard_map/pallas_call | solution.py:379
  68.1 0.8 %copy.7 = bf16[1024,256]{1,0:T(8,128)(2,1)} copy(bf16[1024,256]{1,0:T(8,128)(2,1)S(1)} %shard_map.55) | data formatting | bytes 1048576

commit v4 on v3

--- a/solution.py
+++ b/solution.py
@@ -13,20 +13,26 @@
          (0, 3, 0), (0, 1, 1), (1, 0, 0),
          (1, 0, 1), (0, 2, 0), (0, 2, 1),
          (0, 3, 1), (0, 1, 0),
-         (1, 3, 0), (1, 1, 0), (1, 2, 0), (1, 2, 1),
+         (1, 3, 0), (1, 1, 0),
+         (1, 2, 0), (1, 2, 1),
          (1, 3, 1), (1, 1, 1)]
 UNIT = {b: i for i, b in enumerate(UNITS)}
 QUARTERED = [(0, 3, 0), (0, 1, 1), (1, 0, 0), (1, 3, 1), (1, 1, 1)]
-CHUNKS = {"A": (0, 2), "B": (2, 3), "C": (5, 3), "D": (8, 2), "E": (10, 4), "F": (14, 2)}
+CHUNKS = {"A": (0, 2), "B": (2, 3), "C": (5, 3), "D": (8, 2), "E": (10, 2), "G": (12, 2), "K": (14, 2)}
+ACROSS_Y = "G"
 DESTS = [(1, 2), (1, 1), (1, 3), (0, 2), (1, 0), (0, 1), (0, 3), (0, 0)]
 DEST = {b: i for i, b in enumerate(DESTS)}
 HALF = [[(0, 0, 0), (0, 0, 1), (1, 0, 0), (1, 0, 1)],
-        [(1, 2, 0), (1, 2, 1), (1, 3, 0), (1, 1, 0), (0, 2, 0), (0, 2, 1), (0, 3, 0), (0, 1, 0)],
-        [(0, 3, 1), (0, 1, 1), (1, 3, 1), (1, 1, 1)]]
-ACROSS = [[(0, k, h) for k in range(4) for h in range(2)], [(1, k, 0) for k in range(4)], [(1, k, 1) for k in range(4)]]
-LAST = {link: [[(0, p, 0), (0, p, 1)],
-               [(1, p, 0), (0, m, 0), (0, m, 1), (1, 2, 0), (1, m, 0), (0, 0, 0), (0, 2, 0), (1, 0, 0)],
-               [(1, p, 1), (1, m, 1), (0, 0, 1), (0, 2, 1), (1, 0, 1), (1, 2, 1)]]
+        [(1, 3, 0), (1, 1, 0), (0, 3, 0), (0, 1, 0)],
+        [(1, 2, 0), (1, 2, 1), (0, 2, 0), (0, 2, 1)],
+        [(1, 3, 1), (1, 1, 1), (0, 3, 1), (0, 1, 1)]]
+ACROSS = [[(0, 1, 0), (0, 1, 1), (0, 3, 0), (0, 3, 1)], [(0, 0, 0), (0, 0, 1), (0, 2, 0), (0, 2, 1)],
+          [(1, k, 0) for k in range(4)], [(1, k, 1) for k in range(4)]]
+LAST = {link: [[(0, p, 0), (0, p, 1), (1, p, 0)],
+               [(0, 0, 0), (1, 0, 0)],
+               [(1, p, 1), (1, 2, 0)],
+               [(0, m, 0), (0, m, 1), (1, m, 0), (1, m, 1), (0, 2, 0)],
+               [(0, 0, 1), (0, 2, 1), (1, 0, 1), (1, 2, 1)]]
         for link, p, m in (("zp", 3, 1), ("zm", 1, 3))}
 SEEN = {
     "zp": lambda q, k, h: (q, (k + 1) % 4, h),
@@ -36,7 +42,7 @@
 
 
 def kernel(tok_hbm, gain_ref, gate_hbm, up_hbm, down_hbm, out,
-           x, w, dn, res, hid, own, sb, rb, sd, yl, zl, zh, yf, zf,
+           x, w, dn, res, hid, own, sb, rb, sd, yl, yp, zl, zh, yf, zf,
            tok_sem, w_sem, d_sem, x_sem, pair_sem, sd_sem, rs):
     dp, t = lax.axis_index("dp"), lax.axis_index("tensor")
     hi, z, c = t // 8, lax.rem(t // 2, 4), lax.rem(t, 2)
@@ -88,12 +94,15 @@
     pairs, leaf = {}, {}
     for name, (lo, n) in CHUNKS.items():
         at = rows(lo, n)
-        pairs[name] = [remote("s", sb.at[pl.ds(a, m), at], rb.at[pl.ds(a, m), at], pair_sem) for a, m in ((0, 3), (3, 5))]
-        leaf[name] = {
-            "y": remote("y", sd.at[DEST[1, 2], at], yl.at[at], sd_sem),
-            "zp": remote("zp", sd.at[DEST[1, 1], at], zl.at[0, at], sd_sem),
-            "zm": remote("zm", sd.at[DEST[1, 3], at], zl.at[1, at], sd_sem),
-        }
+        cuts = ((0, 3), (3, 5)) if name in "GK" else ((0, 8),)
+        pairs[name] = [remote("s", sb.at[pl.ds(a, m), at], rb.at[pl.ds(a, m), at], pair_sem) for a, m in cuts]
+        leaf[name] = {"y": remote("y", sd.at[DEST[1, 2], at], yl.at[at], sd_sem)}
+        for link, side, dest in (("zp", 0, (1, 1)), ("zm", 1, (1, 3))):
+            if name == ACROSS_Y:
+                leaf[name][link] = remote("y", sd.at[DEST[dest], at], yp.at[side], sd_sem)
+            else:
+                leaf[name][link] = remote(link, sd.at[DEST[dest], at], zl.at[side, at], sd_sem)
+
     def pieces(orders, make):
         copies, where, at = [], {}, 0
         for i, units in enumerate(orders):
@@ -118,6 +127,10 @@
         if id(copy) not in waited:
             waited.add(id(copy))
             copy.wait_recv()
+
+    def on_y(unit):
+        lo, n = CHUNKS[ACROSS_Y]
+        return lo <= UNIT[unit] < lo + n
 
     def seen_leaf(link, unit):
         at = UNIT[SEEN[link](*unit)]
@@ -189,7 +202,7 @@
         at = UNIT[unit]
         for name, (lo, n) in CHUNKS.items():
             if lo <= at < lo + n:
-                arrived(pairs[name][1 if rest else 0])
+                arrived(pairs[name][-1 if rest else 0])
         return own[r, rows(at, 1)] + rb[r, rows(at, 1)].astype(F32)
 
     def send_leaf(name, links=("y", "zp", "zm")):
@@ -214,8 +227,9 @@
         copies, where = across["y"]
         for unit in ACROSS[i]:
             value = chip_sum(r, unit)
-            value = value + zl[0, seen_leaf("zp", unit)].astype(F32)
-            value = value + zl[1, seen_leaf("zm", unit)].astype(F32)
+            for link, side in (("zp", 0), ("zm", 1)):
+                if not on_y(SEEN[link](*unit)):
+                    value = value + zl[side, seen_leaf(link, unit)].astype(F32)
             sd[r, rows(where[unit][1], 1)] = value.astype(BF16)
         copies[i].start()
 
@@ -225,6 +239,10 @@
             copies, where = last[link]
             for unit in LAST[link][i]:
                 value = chip_sum(r, unit)
+                theirs = SEEN["y"](*unit)
+                if on_y(theirs):
+                    arrived(leaf[ACROSS_Y][link])
+                    value = value + yp[side, rows(UNIT[theirs] - CHUNKS[ACROSS_Y][0], 1)].astype(F32)
                 got = zh[side, seen(half, link, unit)].astype(F32)
                 keep = (1 - side) * 128
                 at = rows(where[unit][1], 1)
@@ -265,10 +283,8 @@
     arrived(y0[0])
     sib[1, 0, 0][0].start()
     pltpu.make_async_copy(dn, dn, d_sem).wait()
-    dot_out(0, 2, 0, 3)
+    dot_out(0, 2, 0, 8)
     pairs["A"][0].start()
-    dot_out(0, 2, 3, 8)
-    pairs["A"][1].start()
     arrived(zp0[1])
     zp2[1].start()
     zp0[3].start()
@@ -285,8 +301,6 @@
     have((0, 3, 0), (0, 1, 1), (1, 0, 0))
     dot_in(2, 3)
     send_leaf("A", ("y",))
-    dot_out(2, 3, 0, 3)
-    pairs["B"][0].start()
     for i in range(2, 4):
         arrived(y0[i])
         zpp[i].start()
@@ -296,8 +310,8 @@
     y2[0].start()
     arrived(zm2[0])
     y2[3].start()
-    dot_out(2, 3, 3, 8)
-    pairs["B"][1].start()
+    dot_out(2, 3, 0, 8)
+    pairs["B"][0].start()
     send_leaf("A", ("zp", "zm"))
     arrived(zp2[1])
     y2[1].start()
@@ -314,55 +328,57 @@
     arrived(zm0[1])
     arrived(zm0[0])
     exchange((0, 1, 0))
-    dot_out(5, 3, 0, 3)
+    dot_out(5, 3, 0, 8)
     pairs["C"][0].start()
-    dot_out(5, 3, 3, 8)
-    pairs["C"][1].start()
-    have((0, 3, 1), (0, 1, 0))
-    dot_in(8, 2)
-    send_leaf("C")
     for copies, unit in ((zpp, (1, 3, 0)), (zmp, (1, 1, 0))):
         arrived(copies[0])
         arrived(copies[1])
         exchange(unit)
-    dot_out(8, 2, 0, 3)
-    pairs["D"][0].start()
-    dot_out(8, 2, 3, 8)
-    pairs["D"][1].start()
-    have((1, 3, 0), (1, 1, 0))
-    dot_in(10, 2)
-    send_leaf("D")
+    have((0, 3, 1), (0, 1, 0))
+    dot_in(8, 2)
+    send_leaf("C")
     for h in range(2):
         arrived(y2[2 * h])
         arrived(y2[2 * h + 1])
         exchange((1, 2, h))
-    have((1, 2, 0), (1, 2, 1))
-    dot_in(12, 2)
+    dot_out(8, 2, 0, 8)
+    pairs["D"][0].start()
+    have((1, 3, 0), (1, 1, 0))
+    dot_in(10, 2)
+    send_leaf("D")
     for i in (2, 3):
         for copies, unit in ((zpp, (1, 3, 1)), (zmp, (1, 1, 1))):
             arrived(copies[i])
             sib[unit][i - 2].start()
-    dot_out(10, 4, 0, 3)
+    dot_out(10, 2, 0, 8)
     pairs["E"][0].start()
+    have((1, 2, 0), (1, 2, 1))
+    dot_in(12, 2)
+    send_leaf("E")
     send_half(0)
-    dot_out(10, 4, 3, 8)
-    pairs["E"][1].start()
-    send_leaf("E")
     send_across(0)
     have((1, 3, 1), (1, 1, 1))
     dot_in(14, 2)
+    dot_out(12, 4, 0, 3)
+    pairs["G"][0].start()
+    pairs["K"][0].start()
+    send_half(1)
+    dot_out(12, 4, 3, 8)
+    pairs["G"][1].start()
+    pairs["K"][1].start()
+    send_leaf("G", ("y",))
+    send_leaf("K")
+    send_across(1)
+    send_leaf("G", ("zp", "zm"))
     send_last(0)
-    dot_out(14, 2, 0, 3)
-    pairs["F"][0].start()
-    send_half(1)
-    dot_out(14, 2, 3, 8)
-    pairs["F"][1].start()
-    send_leaf("F")
-    send_across(1)
     send_last(1)
     send_half(2)
+    send_half(3)
+    send_last(2)
     send_across(2)
-    send_last(2)
+    send_across(3)
+    send_last(3)
+    send_last(4)
     piece = {u: max(last[link][1][SEEN[link](*u)][0] for link in ("zp", "zm")) for u in UNITS}
     for unit in sorted(UNITS, key=lambda u: piece[u]):
         finish(unit)
@@ -371,7 +387,7 @@
     all_sent(sd, sd_sem)
 
 
-N_REMOTE = 28 + 16 + 5 + 6 * 5 + 15
+N_REMOTE = 28 + 16 + 5 + 9 + 7 * 3 + 8 + 4 + 10
 ANY, VMEM = pl.BlockSpec(memory_space=pl.ANY), pl.BlockSpec(memory_space=pltpu.VMEM)
 
 
@@ -392,6 +408,7 @@
             pltpu.VMEM((8, ROWS, COLS), BF16),
             pltpu.VMEM((7, ROWS, COLS), BF16),
             pltpu.VMEM((ROWS, COLS), BF16),
+            pltpu.VMEM((2, 128, COLS), BF16),
             pltpu.VMEM((2, ROWS, COLS), BF16),
             pltpu.VMEM((2, ROWS, 128), BF16),
             pltpu.VMEM((ROWS, COLS), BF16),

time: 69.5 us -> 69.3 us (level)
  no operation moved by 1% of the time
where the time goes in v4:
time: 69.3 us; the launch traced here: 69.1 us
  Pallas kernels  68.3 us (99%)
  local copies, waits for them, and re-layouts  0.8 us (1%)
    pallas_call x1, Pallas kernels, on_device(): pl.pallas_call(kernel, out_shape=pltpu.VMEM((ROWS, COLS), BF16), in_specs...  68.3 us

profile of v4, /device:TPU:0, one launch (start us, length us, event | category | flops | bytes accessed | tf_op | source)
XLA Modules:
  0.0 69.1 jit_solution(2585300188013306404)
XLA Ops:
  0.0 68.3 %shard_map.55 = bf16[1024,256]{1,0:T(8,128)(2,1)S(1)} custom-call(bf16[4,16,4096]{2,1,0:T(8,128)(2,1)} %bitcast.2, f32[1,4096]{1,0:T(1,128)} %bitcast.3, bf16[4096,896]{1,0:T(8,128)(2,1)} %gate_hbm.1, bf16[4096,896]{1,0:T(8,128)(2,1)} %up_hbm.1, bf16[896,4096]{1,0:T(8,128)(2,1)} %down_hbm.1), custom_call_target="tpu_custom_call" | custom-call | tf_op jit(solution)/shard_map/pallas_call | solution.py:395
  68.3 0.8 %copy.7 = bf16[1024,256]{1,0:T(8,128)(2,1)} copy(bf16[1024,256]{1,0:T(8,128)(2,1)S(1)} %shard_map.55) | data formatting | bytes 1048576

commit v5 on v4

--- a/solution.py
+++ b/solution.py
@@ -17,22 +17,24 @@
          (1, 2, 0), (1, 2, 1),
          (1, 3, 1), (1, 1, 1)]
 UNIT = {b: i for i, b in enumerate(UNITS)}
-QUARTERED = [(0, 3, 0), (0, 1, 1), (1, 0, 0), (1, 3, 1), (1, 1, 1)]
+QUARTERED = [(0, 3, 0), (0, 1, 1), (1, 0, 0), (0, 2, 0), (0, 2, 1),
+             (1, 3, 0), (1, 1, 0), (1, 2, 0), (1, 2, 1)]
 CHUNKS = {"A": (0, 2), "B": (2, 3), "C": (5, 3), "D": (8, 2), "E": (10, 2), "G": (12, 2), "K": (14, 2)}
-ACROSS_Y = "G"
+ACROSS_Y = "DG"
 DESTS = [(1, 2), (1, 1), (1, 3), (0, 2), (1, 0), (0, 1), (0, 3), (0, 0)]
 DEST = {b: i for i, b in enumerate(DESTS)}
 HALF = [[(0, 0, 0), (0, 0, 1), (1, 0, 0), (1, 0, 1)],
         [(1, 3, 0), (1, 1, 0), (0, 3, 0), (0, 1, 0)],
         [(1, 2, 0), (1, 2, 1), (0, 2, 0), (0, 2, 1)],
         [(1, 3, 1), (1, 1, 1), (0, 3, 1), (0, 1, 1)]]
-ACROSS = [[(0, 1, 0), (0, 1, 1), (0, 3, 0), (0, 3, 1)], [(0, 0, 0), (0, 0, 1), (0, 2, 0), (0, 2, 1)],
-          [(1, k, 0) for k in range(4)], [(1, k, 1) for k in range(4)]]
-LAST = {link: [[(0, p, 0), (0, p, 1), (1, p, 0)],
+ACROSS = [[(0, 0, 0), (0, 0, 1), (0, 2, 0), (0, 2, 1)], [(0, 1, 0), (0, 1, 1), (0, 3, 0), (0, 3, 1)],
+          [(1, 0, 0), (1, 1, 0), (1, 3, 0), (1, 2, 0)], [(1, 0, 1), (1, 1, 1), (1, 3, 1), (1, 2, 1)]]
+LAST = {link: [[(0, p, 0), (0, p, 1)],
+               [(1, p, 0)],
                [(0, 0, 0), (1, 0, 0)],
                [(1, p, 1), (1, 2, 0)],
-               [(0, m, 0), (0, m, 1), (1, m, 0), (1, m, 1), (0, 2, 0)],
-               [(0, 0, 1), (0, 2, 1), (1, 0, 1), (1, 2, 1)]]
+               [(0, m, 0), (0, m, 1), (1, m, 0), (1, m, 1)],
+               [(0, 0, 1), (1, 0, 1), (1, 2, 1), (0, 2, 0), (0, 2, 1)]]
         for link, p, m in (("zp", 3, 1), ("zm", 1, 3))}
 SEEN = {
     "zp": lambda q, k, h: (q, (k + 1) % 4, h),
@@ -98,8 +100,8 @@
         pairs[name] = [remote("s", sb.at[pl.ds(a, m), at], rb.at[pl.ds(a, m), at], pair_sem) for a, m in cuts]
         leaf[name] = {"y": remote("y", sd.at[DEST[1, 2], at], yl.at[at], sd_sem)}
         for link, side, dest in (("zp", 0, (1, 1)), ("zm", 1, (1, 3))):
-            if name == ACROSS_Y:
-                leaf[name][link] = remote("y", sd.at[DEST[dest], at], yp.at[side], sd_sem)
+            if name in ACROSS_Y:
+                leaf[name][link] = remote("y", sd.at[DEST[dest], at], yp.at[ACROSS_Y.index(name), side], sd_sem)
             else:
                 leaf[name][link] = remote(link, sd.at[DEST[dest], at], zl.at[side, at], sd_sem)
 
@@ -129,8 +131,7 @@
             copy.wait_recv()
 
     def on_y(unit):
-        lo, n = CHUNKS[ACROSS_Y]
-        return lo <= UNIT[unit] < lo + n
+        return [name for name in ACROSS_Y if CHUNKS[name][0] <= UNIT[unit] < sum(CHUNKS[name])]
 
     def seen_leaf(link, unit):
         at = UNIT[SEEN[link](*unit)]
@@ -165,17 +166,12 @@
     pl.semaphore_wait(barrier, 4)
 
     exchange((0, 0, 0), (0, 0, 1))
-    for i in range(3):
+    for i in range(2):
         zp0[i].start()
         zm0[3 - i].start()
         y0[i].start()
+    y0[2].start()
     y0[3].start()
-    for r, (q, k) in enumerate(DESTS):
-        for part, core in enumerate((1 - c, c)):
-            col = pl.multiple_of(member(q, k, core) * COLS, COLS)
-            pltpu.make_async_copy(
-                down_hbm.at[:, pl.ds(col, COLS)], dn.at[:, pl.ds((2 * r + part) * COLS, COLS)], d_sem).start()
-
     def dot_in(lo, n):
         both = jnp.dot(x[pl.ds(lo, n)].reshape(n * 64, D), w[...], preferred_element_type=F32)
         for j in range(7):
@@ -240,9 +236,10 @@
             for unit in LAST[link][i]:
                 value = chip_sum(r, unit)
                 theirs = SEEN["y"](*unit)
-                if on_y(theirs):
-                    arrived(leaf[ACROSS_Y][link])
-                    value = value + yp[side, rows(UNIT[theirs] - CHUNKS[ACROSS_Y][0], 1)].astype(F32)
+                for name in on_y(theirs):
+                    arrived(leaf[name][link])
+                    part = yp[ACROSS_Y.index(name), side, rows(UNIT[theirs] - CHUNKS[name][0], 1)]
+                    value = value + part.astype(F32)
                 got = zh[side, seen(half, link, unit)].astype(F32)
                 keep = (1 - side) * 128
                 at = rows(where[unit][1], 1)
@@ -273,6 +270,11 @@
 
     have((0, 0, 0), (0, 0, 1))
     pltpu.make_async_copy(w, w, w_sem).wait()
+    for r, (q, k) in enumerate(DESTS):
+        for part, core in enumerate((1 - c, c)):
+            col = pl.multiple_of(member(q, k, core) * COLS, COLS)
+            pltpu.make_async_copy(
+                down_hbm.at[:, pl.ds(col, COLS)], dn.at[:, pl.ds((2 * r + part) * COLS, COLS)], d_sem).start()
     dot_in(0, 2)
     arrived(zp0[0])
     zp2[0].start()
@@ -282,15 +284,14 @@
     sib[0, 1, 1][1].start()
     arrived(y0[0])
     sib[1, 0, 0][0].start()
-    pltpu.make_async_copy(dn, dn, d_sem).wait()
-    dot_out(0, 2, 0, 8)
-    pairs["A"][0].start()
     arrived(zp0[1])
     zp2[1].start()
+    zp0[2].start()
     zp0[3].start()
     sib[0, 3, 0][1].start()
     arrived(zm0[2])
     zm2[1].start()
+    zm0[1].start()
     zm0[0].start()
     sib[0, 1, 1][0].start()
     arrived(y0[1])
@@ -298,88 +299,100 @@
     for i in range(2):
         zpp[i].start()
         zmp[i].start()
+    pltpu.make_async_copy(dn, dn, d_sem).wait()
+    dot_out(0, 2, 0, 8)
+    pairs["A"][0].start()
     have((0, 3, 0), (0, 1, 1), (1, 0, 0))
     dot_in(2, 3)
-    send_leaf("A", ("y",))
+    arrived(zp2[0])
+    y2[0].start()
+    sib[0, 2, 0][0].start()
+    arrived(zm2[0])
+    y2[3].start()
+    sib[0, 2, 1][1].start()
+    dot_out(2, 3, 0, 3)
+    arrived(zp2[1])
+    y2[1].start()
+    sib[0, 2, 0][1].start()
+    arrived(zm2[1])
+    y2[2].start()
+    sib[0, 2, 1][0].start()
+    arrived(y0[2])
+    arrived(y0[3])
+    exchange((1, 0, 1))
+    dot_out(2, 3, 3, 8)
+    pairs["B"][0].start()
+    send_leaf("A")
+    have((1, 0, 1), (0, 2, 0), (0, 2, 1))
+    dot_in(5, 3)
+    send_leaf("B")
     for i in range(2, 4):
-        arrived(y0[i])
         zpp[i].start()
         zmp[i].start()
-    exchange((1, 0, 1))
-    arrived(zp2[0])
-    y2[0].start()
-    arrived(zm2[0])
-    y2[3].start()
-    dot_out(2, 3, 0, 8)
-    pairs["B"][0].start()
-    send_leaf("A", ("zp", "zm"))
-    arrived(zp2[1])
-    y2[1].start()
-    exchange((0, 2, 0))
-    arrived(zm2[1])
-    y2[2].start()
-    exchange((0, 2, 1))
-    send_leaf("B")
-    have((1, 0, 1), (0, 2, 0), (0, 2, 1))
-    dot_in(5, 3)
+    dot_out(5, 3, 0, 3)
     arrived(zp0[2])
     arrived(zp0[3])
     exchange((0, 3, 1))
     arrived(zm0[1])
     arrived(zm0[0])
     exchange((0, 1, 0))
-    dot_out(5, 3, 0, 8)
+    dot_out(5, 3, 3, 8)
     pairs["C"][0].start()
-    for copies, unit in ((zpp, (1, 3, 0)), (zmp, (1, 1, 0))):
-        arrived(copies[0])
-        arrived(copies[1])
-        exchange(unit)
     have((0, 3, 1), (0, 1, 0))
     dot_in(8, 2)
     send_leaf("C")
-    for h in range(2):
-        arrived(y2[2 * h])
-        arrived(y2[2 * h + 1])
-        exchange((1, 2, h))
+    for copies, unit in ((zpp, (1, 3, 0)), (zmp, (1, 1, 0))):
+        arrived(copies[0])
+        sib[unit][0].start()
     dot_out(8, 2, 0, 8)
+    for copies, unit in ((zpp, (1, 3, 0)), (zmp, (1, 1, 0))):
+        arrived(copies[1])
+        sib[unit][1].start()
     pairs["D"][0].start()
     have((1, 3, 0), (1, 1, 0))
+    for i in (0, 3, 1, 2):
+        arrived(y2[i])
+        sib[1, 2, i // 2][i % 2].start()
     dot_in(10, 2)
+    send_across(0)
     send_leaf("D")
-    for i in (2, 3):
-        for copies, unit in ((zpp, (1, 3, 1)), (zmp, (1, 1, 1))):
-            arrived(copies[i])
-            sib[unit][i - 2].start()
     dot_out(10, 2, 0, 8)
     pairs["E"][0].start()
+    send_half(0)
     have((1, 2, 0), (1, 2, 1))
     dot_in(12, 2)
+    for copies, unit in ((zpp, (1, 3, 1)), (zmp, (1, 1, 1))):
+        arrived(copies[2])
+        arrived(copies[3])
+        exchange(unit)
     send_leaf("E")
-    send_half(0)
-    send_across(0)
+    dot_out(12, 2, 0, 3)
+    pairs["G"][0].start()
+    send_last(0)
+    dot_out(12, 2, 3, 8)
+    pairs["G"][1].start()
+    send_leaf("G", ("y",))
+    send_across(1)
     have((1, 3, 1), (1, 1, 1))
     dot_in(14, 2)
-    dot_out(12, 4, 0, 3)
-    pairs["G"][0].start()
+    send_half(1)
+    send_last(1)
+    dot_out(14, 2, 0, 3)
     pairs["K"][0].start()
-    send_half(1)
-    dot_out(12, 4, 3, 8)
-    pairs["G"][1].start()
+    dot_out(14, 2, 3, 8)
     pairs["K"][1].start()
-    send_leaf("G", ("y",))
+    send_half(2)
     send_leaf("K")
-    send_across(1)
     send_leaf("G", ("zp", "zm"))
-    send_last(0)
-    send_last(1)
-    send_half(2)
+    send_last(2)
+    send_last(3)
+    send_across(2)
     send_half(3)
-    send_last(2)
-    send_across(2)
+    send_last(4)
     send_across(3)
-    send_last(3)
-    send_last(4)
-    piece = {u: max(last[link][1][SEEN[link](*u)][0] for link in ("zp", "zm")) for u in UNITS}
+    send_last(5)
+    sent = (0, 1, 2, 3, 4, 5)
+    piece = {u: max(sent.index(last[link][1][SEEN[link](*u)][0]) for link in ("zp", "zm")) for u in UNITS}
     for unit in sorted(UNITS, key=lambda u: piece[u]):
         finish(unit)
     all_sent(x.at[pl.ds(0, 15)], x_sem)
@@ -387,7 +400,7 @@
     all_sent(sd, sd_sem)
 
 
-N_REMOTE = 28 + 16 + 5 + 9 + 7 * 3 + 8 + 4 + 10
+N_REMOTE = 28 + 16 + 9 + 9 + 7 * 3 + 8 + 4 + 12
 ANY, VMEM = pl.BlockSpec(memory_space=pl.ANY), pl.BlockSpec(memory_space=pltpu.VMEM)
 
 
@@ -408,7 +421,7 @@
             pltpu.VMEM((8, ROWS, COLS), BF16),
             pltpu.VMEM((7, ROWS, COLS), BF16),
             pltpu.VMEM((ROWS, COLS), BF16),
-            pltpu.VMEM((2, 128, COLS), BF16),
+            pltpu.VMEM((2, 2, 128, COLS), BF16),
             pltpu.VMEM((2, ROWS, COLS), BF16),
             pltpu.VMEM((2, ROWS, 128), BF16),
             pltpu.VMEM((ROWS, COLS), BF16),

time: 69.3 us -> 68.7 us (level)
  Pallas kernels: 68.3 us -> 67.4 us
    pallas_call x1, Pallas kernels: 68.3 us -> 67.4 us  [on_device(): pl.pallas_call(kernel, out_shape=pltpu.VMEM((ROWS, COLS), BF16), in_specs...]
where the time goes in v5:
time: 68.7 us; the launch traced here: 68.2 us
  Pallas kernels  67.4 us (98%)
  local copies, waits for them, and re-layouts  0.8 us (1%)
    pallas_call x1, Pallas kernels, on_device(): pl.pallas_call(kernel, out_shape=pltpu.VMEM((ROWS, COLS), BF16), in_specs...  67.4 us

profile of v5, /device:TPU:0, one launch (start us, length us, event | category | flops | bytes accessed | tf_op | source)
XLA Modules:
  0.0 68.2 jit_solution(1888547263730070515)
XLA Ops:
  0.0 67.4 %shard_map.55 = bf16[1024,256]{1,0:T(8,128)(2,1)S(1)} custom-call(bf16[4,16,4096]{2,1,0:T(8,128)(2,1)} %bitcast.2, f32[1,4096]{1,0:T(1,128)} %bitcast.3, bf16[4096,896]{1,0:T(8,128)(2,1)} %gate_hbm.1, bf16[4096,896]{1,0:T(8,128)(2,1)} %up_hbm.1, bf16[896,4096]{1,0:T(8,128)(2,1)} %down_hbm.1), custom_call_target="tpu_custom_call" | custom-call | tf_op jit(solution)/shard_map/pallas_call | solution.py:408
  67.4 0.8 %copy.7 = bf16[1024,256]{1,0:T(8,128)(2,1)} copy(bf16[1024,256]{1,0:T(8,128)(2,1)S(1)} %shard_map.55) | data formatting | bytes 1048576

commit v6 on v5

--- a/solution.py
+++ b/solution.py
@@ -353,8 +353,8 @@
     for i in (0, 3, 1, 2):
         arrived(y2[i])
         sib[1, 2, i // 2][i % 2].start()
+    send_across(0)
     dot_in(10, 2)
-    send_across(0)
     send_leaf("D")
     dot_out(10, 2, 0, 8)
     pairs["E"][0].start()
@@ -368,10 +368,10 @@
     send_leaf("E")
     dot_out(12, 2, 0, 3)
     pairs["G"][0].start()
-    send_last(0)
     dot_out(12, 2, 3, 8)
     pairs["G"][1].start()
     send_leaf("G", ("y",))
+    send_last(0)
     send_across(1)
     have((1, 3, 1), (1, 1, 1))
     dot_in(14, 2)

time: 68.7 us -> 68.4 us (level)
  no operation moved by 1% of the time
where the time goes in v6:
time: 68.4 us; the launch traced here: 68.2 us
  Pallas kernels  67.4 us (99%)
  local copies, waits for them, and re-layouts  0.8 us (1%)
    pallas_call x1, Pallas kernels, on_device(): pl.pallas_call(kernel, out_shape=pltpu.VMEM((ROWS, COLS), BF16), in_specs...  67.4 us

profile of v6, /device:TPU:0, one launch (start us, length us, event | category | flops | bytes accessed | tf_op | source)
XLA Modules:
  0.0 68.2 jit_solution(5409034908741276257)
XLA Ops:
  0.0 67.4 %shard_map.55 = bf16[1024,256]{1,0:T(8,128)(2,1)S(1)} custom-call(bf16[4,16,4096]{2,1,0:T(8,128)(2,1)} %bitcast.2, f32[1,4096]{1,0:T(1,128)} %bitcast.3, bf16[4096,896]{1,0:T(8,128)(2,1)} %gate_hbm.1, bf16[4096,896]{1,0:T(8,128)(2,1)} %up_hbm.1, bf16[896,4096]{1,0:T(8,128)(2,1)} %down_hbm.1), custom_call_target="tpu_custom_call" | custom-call | tf_op jit(solution)/shard_map/pallas_call | solution.py:408
  67.4 0.8 %copy.7 = bf16[1024,256]{1,0:T(8,128)(2,1)} copy(bf16[1024,256]{1,0:T(8,128)(2,1)S(1)} %shard_map.55) | data formatting | bytes 1048576

commit v7 on v6

--- a/solution.py
+++ b/solution.py
@@ -275,7 +275,6 @@
             col = pl.multiple_of(member(q, k, core) * COLS, COLS)
             pltpu.make_async_copy(
                 down_hbm.at[:, pl.ds(col, COLS)], dn.at[:, pl.ds((2 * r + part) * COLS, COLS)], d_sem).start()
-    dot_in(0, 2)
     arrived(zp0[0])
     zp2[0].start()
     sib[0, 3, 0][0].start()
@@ -284,6 +283,7 @@
     sib[0, 1, 1][1].start()
     arrived(y0[0])
     sib[1, 0, 0][0].start()
+    dot_in(0, 2)
     arrived(zp0[1])
     zp2[1].start()
     zp0[2].start()

time: 68.4 us -> 68.4 us (level)
  no operation moved by 1% of the time
where the time goes in v7:
time: 68.4 us; the launch traced here: 68.2 us
  Pallas kernels  67.4 us (99%)
  local copies, waits for them, and re-layouts  0.8 us (1%)
    pallas_call x1, Pallas kernels, on_device(): pl.pallas_call(kernel, out_shape=pltpu.VMEM((ROWS, COLS), BF16), in_specs...  67.4 us

profile of v7, /device:TPU:0, one launch (start us, length us, event | category | flops | bytes accessed | tf_op | source)
XLA Modules:
  0.0 68.2 jit_solution(16248914583281566915)
XLA Ops:
  0.0 67.4 %shard_map.55 = bf16[1024,256]{1,0:T(8,128)(2,1)S(1)} custom-call(bf16[4,16,4096]{2,1,0:T(8,128)(2,1)} %bitcast.2, f32[1,4096]{1,0:T(1,128)} %bitcast.3, bf16[4096,896]{1,0:T(8,128)(2,1)} %gate_hbm.1, bf16[4096,896]{1,0:T(8,128)(2,1)} %up_hbm.1, bf16[896,4096]{1,0:T(8,128)(2,1)} %down_hbm.1), custom_call_target="tpu_custom_call" | custom-call | tf_op jit(solution)/shard_map/pallas_call | solution.py:408
  67.4 0.8 %copy.7 = bf16[1024,256]{1,0:T(8,128)(2,1)} copy(bf16[1024,256]{1,0:T(8,128)(2,1)S(1)} %shard_map.55) | data formatting | bytes 1048576
